TPU v7x, 128 devices: a whole 4x4x4 slice. The times are simulated.
128 devices in a mesh: rows: 32 (over y, x, core), gz: 4 (over z).
Axes of the slice: x: 4, y: 4, z: 4, core: 2. Of those that a mesh axis runs over, the one named last changes fastest.
Arguments:
- segment_warming: float32 [64, 1024, 1024], P('gz', 'rows'), may hold values from 0.15 to 3
- eigenfunction_crosssections: float32 [10, 1024, 1024], P(None, 'rows'), may hold values from -2.5 to 2.5
- segment_phasors: float32 [64, 10], P('gz'), may hold values from 0.2 to 2
- injected_coefficients: float32 [2, 10], replicated, may hold values from -6 to 6
Outputs:
- diffused_warmth: float32 [64, 1024, 1024], P('gz', 'rows')
- refreshed_coupling_sums: float32 [64, 10, 10], P('gz')
- incoming_coefficients: float32 [64, 2, 10], P('gz')
All inputs are finite; a program needn't handle non-finite values.
Results may differ from a plain program's by a relative error of at most 0.0003.
Values sent between devices are 32-bit elements; how exact they have to be, the bound alone decides.
No kernel may reach another device: no remote copies, remote signals or barrier semaphores. Data moves between devices by JAX's collectives and lax.ppermute only.
A program may use at most 128 MiB of HBM per device.

v0:
```python
import jax
import jax.numpy as jnp
import numpy as np
from jax import lax
from jax.experimental import pallas as pl
from jax.experimental.pallas import tpu as pltpu
from jax.sharding import PartitionSpec as P

NX = 1024
NY = 1024
M = 10
PASSES = 16
ROWS = 32
HALO = 16
WIDE = ROWS + 2 * HALO
ZL = 16
GZ = 4
TILES = NY // 128
BLOCK = 8
TALL = WIDE + BLOCK
highest = lax.Precision.HIGHEST
f32 = jnp.float32
bf16 = jnp.bfloat16


def pair_modes():
    table = []
    for group in range(8):
        for sub in range(8):
            if group < 3:
                table.append((group, sub))
            elif group == 3:
                table.append(((8, 8), (8, 9), (9, 9))[sub] if sub < 3 else (3, sub))
            elif group < 6:
                first = 4 + 2 * (group - 4)
                table.append((first, 4 + sub) if sub < 4 else (first + 1, sub))
            else:
                table.append((group + 2, sub))
    return table


def selection(stride, rows):
    where = {}
    for row, (m, n) in enumerate(pair_modes()):
        where.setdefault((m, n), row)
        where.setdefault((n, m), row)
    chosen = np.zeros((rows, 64), np.float32)
    for i in range(M):
        for j in range(M):
            chosen[i * stride + j, where[(i, j)]] = 1.0
    return chosen


def diagonal_rows():
    table = pair_modes()
    return [table.index((m, m)) for m in range(M)]


def split(value):
    high = value.astype(bf16)
    low = (value - high.astype(f32)).astype(bf16)
    return high, low


def pair_products(modes_ref, row):
    low = modes_ref[row, 0:8, :]
    sub = lax.broadcasted_iota(jnp.int32, (8, NY), 0)

    def mode(m):
        return jnp.broadcast_to(modes_ref[row, m : m + 1, :], (8, NY))

    m8, m9 = mode(8), mode(9)
    turned = jnp.where(sub < 4, pltpu.roll(low, 4, 0), low)
    left3 = jnp.where(sub < 2, m8, jnp.where(sub == 2, m9, mode(3)))
    right3 = jnp.where(sub == 0, m8, jnp.where(sub < 3, m9, low))
    groups = [
        mode(0) * low,
        mode(1) * low,
        mode(2) * low,
        left3 * right3,
        jnp.where(sub < 4, mode(4), mode(5)) * turned,
        jnp.where(sub < 4, mode(6), mode(7)) * turned,
        m8 * low,
        m9 * low,
    ]
    return jnp.concatenate(groups, axis=0)


def sums_of_rows(field_ref, modes_ref, first, unroll):
    def step(r, acc):
        products = jnp.concatenate(split(pair_products(modes_ref, first + r)), axis=0)
        warmth = jnp.concatenate(split(field_ref[first + r]), axis=0)
        return acc + lax.dot_general(
            products, warmth, (((1,), (1,)), ((), ())), preferred_element_type=f32
        )

    return lax.fori_loop(0, ROWS, step, jnp.zeros((128, 32), f32), unroll=unroll)


def packed_sums(acc, pad_ref, scale, extra):
    pad_ref[...] = jnp.zeros((128, 128), f32)
    pad_ref[:, 0:32] = acc
    both = pad_ref[0:64, :] + pad_ref[64:128, :]
    total = (both + pltpu.roll(both, 112, 1)) * scale
    lane = lax.broadcasted_iota(jnp.int32, (64, 128), 1)
    total = jnp.where(lane < ZL, total, 0.0)
    if extra is not None:
        total = total + extra
    packed = total[0:8]
    for group in range(1, 8):
        packed = packed + pltpu.roll(total[8 * group : 8 * group + 8], 16 * group, 1)
    return packed


def start_sums(w, e, ph, out, wt, et, pad, wsem, esem):
    copies = []
    for z in range(ZL):
        copies.append(pltpu.make_async_copy(w.at[z], wt.at[:, z, :], wsem.at[z]))
    for m in range(M):
        copies.append(pltpu.make_async_copy(e.at[m], et.at[:, m, :], esem.at[m]))
    for copy in copies:
        copy.start()
    pad[...] = jnp.zeros((128, 128), f32)
    pad[0:ZL, 0:M] = ph[...]
    turned = pad[...].T
    row = lax.broadcasted_iota(jnp.int32, (64, 128), 0)
    phases = jnp.zeros((64, 128), f32)
    for m, place in enumerate(diagonal_rows()):
        phases = phases + jnp.where(
            row == place, jnp.broadcast_to(turned[m : m + 1, :], (64, 128)), 0.0
        )
    phases = phases * jnp.where(lax.axis_index("rows") == 0, 1.0, 0.0)
    for copy in copies:
        copy.wait()
    acc = sums_of_rows(wt, et, 0, 16)
    packed = packed_sums(acc, pad, 2.0 / float(NX * NY), phases)
    out[...] = jnp.broadcast_to(packed[None], out.shape)


def three_parts(value):
    first = value.astype(bf16)
    rest = value - first.astype(f32)
    second = rest.astype(bf16)
    third = (rest - second.astype(f32)).astype(bf16)
    return jnp.concatenate([first, second, third], axis=0)


def lane_order():
    column = np.arange(NY)
    order = np.zeros((NY, NY), np.float32)
    order[column, (column % TILES) * 128 + column // TILES] = 1.0
    return order


def permuted(value, order_ref, back):
    count = value.shape[0]
    moved = lax.dot_general(
        three_parts(value),
        order_ref[...],
        (((1,), (1 if back else 0,)), ((), ())),
        preferred_element_type=f32,
    )
    return (moved[0:count] + moved[count : 2 * count]) + moved[2 * count :]


def reorder(w, e, order, unused, full, low, high, raw, moved, lsem, ssem):
    loads = [
        pltpu.make_async_copy(w, raw.at[0:ZL], lsem.at[0]),
        pltpu.make_async_copy(e, raw.at[ZL : ZL + M], lsem.at[1]),
    ]
    for copy in loads:
        copy.start()
    for copy in loads:
        copy.wait()
    stores = []
    for part, (start, stop) in enumerate(((0, 8), (8, 16), (16, 21), (21, 26))):
        rows = (stop - start) * ROWS
        block = raw[start:stop].reshape(rows, NY)
        moved[start:stop] = permuted(block, order, False).reshape(stop - start, ROWS, NY)
        here = slice(start, stop)
        stores += [
            pltpu.make_async_copy(
                moved.at[here, ROWS - HALO : ROWS, :], low.at[here], ssem.at[part, 0]
            ),
            pltpu.make_async_copy(moved.at[here, 0:HALO, :], high.at[here], ssem.at[part, 1]),
            pltpu.make_async_copy(moved.at[here], full.at[here], ssem.at[part, 2]),
        ]
        for copy in stores[-3:]:
            copy.start()
    for copy in stores:
        copy.wait()


def row_of(ref, *index):
    return jnp.broadcast_to(ref[index], (16, 128))


def amplitudes(parts, pick, v0, cs, ts, square, incoming):
    lane8 = lax.broadcasted_iota(jnp.int32, (8, 128), 1)
    totals = []
    for q in range(GZ):
        total = parts[q]
        for r in range(1, 32):
            total = total + parts[GZ * r + q]
        totals.append(total)
    rows = []
    for group in range(8):
        merged = jnp.zeros((8, 128), f32)
        for q in range(GZ):
            moved = pltpu.roll(totals[q], (16 * q - 16 * group) % 128, 1)
            merged = jnp.where(lane8 // ZL == q, moved, merged)
        rows.append(merged)
    pairs = jnp.concatenate(rows, axis=0)
    cs[...] = jnp.dot(pick[...], pairs, precision=highest, preferred_element_type=f32)

    sub = lax.broadcasted_iota(jnp.int32, (16, 128), 0)
    lane = lax.broadcasted_iota(jnp.int32, (16, 128), 1)
    coupled = [cs[16 * i : 16 * i + 16, :] for i in range(M)]
    matrix = []
    right = []
    for i in range(M):
        total = jnp.where(sub == i, 1.0, 0.0)
        for k in range(M):
            total = total + row_of(cs, pl.ds(16 * i + k, 1), slice(None)) * coupled[k]
        matrix.append(total)
        right.append(2.0 * coupled[i])
    for k in range(M):
        pivot = 1.0 / matrix[k][k : k + 1, :]
        pivot = jnp.broadcast_to(pivot, (16, 128))
        row_m = jnp.where(sub == k, pivot, matrix[k] * pivot)
        row_b = right[k] * pivot
        for i in range(M):
            if i != k:
                factor = jnp.broadcast_to(matrix[i][k : k + 1, :], (16, 128))
                matrix[i] = jnp.where(sub == k, 0.0, matrix[i]) - factor * row_m
                right[i] = right[i] - factor * row_b
        matrix[k] = row_m
        right[k] = row_b
    for i in range(M):
        ts[0, 0, 16 * i : 16 * i + 16, :] = 2.0 * matrix[i] - jnp.where(sub == i, 1.0, 0.0)
        ts[0, 1, 16 * i : 16 * i + 16, :] = right[i]

    for level in range(1, 6):
        back = 128 - (1 << (level - 1))
        later_r = [
            pltpu.roll(ts[level - 1, 0, 16 * j : 16 * j + 16, :], back, 1) for j in range(M)
        ]
        later_i = [
            pltpu.roll(ts[level - 1, 1, 16 * j : 16 * j + 16, :], back, 1) for j in range(M)
        ]
        for k in range(M):
            real = jnp.zeros((16, 128), f32)
            imag = jnp.zeros((16, 128), f32)
            for j in range(M):
                er = row_of(ts, level - 1, 0, pl.ds(16 * k + j, 1), slice(None))
                ei = row_of(ts, level - 1, 1, pl.ds(16 * k + j, 1), slice(None))
                real = real + (er * later_r[j] - ei * later_i[j])
                imag = imag + (er * later_i[j] + ei * later_r[j])
            ts[level, 0, 16 * k : 16 * k + 16, :] = real
            ts[level, 1, 16 * k : 16 * k + 16, :] = imag

    vr = jnp.zeros((16, 128), f32)
    vi = jnp.zeros((16, 128), f32)
    for m in range(M):
        spot = (sub == m) & (lane == 0)
        vr = jnp.where(spot, v0[0, m], vr)
        vi = jnp.where(spot, v0[1, m], vi)
    for level in range(5, -1, -1):
        half = 1 << level
        yr = jnp.zeros((16, 128), f32)
        yi = jnp.zeros((16, 128), f32)
        for k in range(M):
            tr = ts[level, 0, 16 * k : 16 * k + 16, :]
            ti = ts[level, 1, 16 * k : 16 * k + 16, :]
            ar = jnp.broadcast_to(vr[k : k + 1, :], (16, 128))
            ai = jnp.broadcast_to(vi[k : k + 1, :], (16, 128))
            yr = yr + (tr * ar - ti * ai)
            yi = yi + (tr * ai + ti * ar)
        target = lane % (2 * half) == half
        vr = jnp.where(target, pltpu.roll(yr, half, 1), vr)
        vi = jnp.where(target, pltpu.roll(yi, half, 1), vi)

    turn = (128 - ZL * lax.axis_index("gz")) % 128
    square[...] = jnp.zeros((128, 128), f32)
    vr = pltpu.roll(vr, turn, 1)
    vi = pltpu.roll(vi, turn, 1)
    incoming[:, 0, :] = vr[0:M, 0:ZL]
    incoming[:, 1, :] = vi[0:M, 0:ZL]
    square[0:16, :] = vr
    square[16:32, :] = vi
    turned = square[...].T[0:ZL, :]
    real = jnp.where(lane < 16, turned, 0.0)
    imag = jnp.where(lane < 16, pltpu.roll(turned, 112, 1), 0.0)
    return real, imag


def heat_load(real, imag, modes_ref, source_ref):
    both = jnp.concatenate([real, imag], axis=0)
    high = both.astype(bf16).astype(f32)
    low = both - high
    weights = high + pltpu.roll(high, 16, 1) + pltpu.roll(low, 32, 1) + pltpu.roll(low, 48, 1)
    weights = weights[:, 0:64].astype(bf16)

    def step(r, unused):
        high_e, low_e = split(modes_ref[r])
        stacked = jnp.concatenate([high_e, low_e, high_e, low_e], axis=0)
        field = jnp.dot(weights, stacked, preferred_element_type=f32)
        re, im = field[0:16], field[16:32]
        source_ref[r] = 0.01 * (re * re + im * im)
        return unused

    lax.fori_loop(0, WIDE, step, 0, unroll=16)


def one_pass(old, new, source, number):
    lane = lax.broadcasted_iota(jnp.int32, (8, 128), 1)
    first_lane = lane == 0
    last_lane = lane == 127

    def block(b, unused):
        r = number + BLOCK * b
        for half in range(2):
            z = slice(8 * half, 8 * half + 8)
            rows = [
                [old[r - 1 + i, z, 128 * t : 128 * t + 128] for t in range(TILES)]
                for i in range(BLOCK + 2)
            ]
            for i in range(BLOCK):
                center = rows[i + 1]
                before = jnp.where(first_lane, 0.0, pltpu.roll(center[TILES - 1], 1, 1))
                after = jnp.where(last_lane, 0.0, pltpu.roll(center[0], 127, 1))
                for t in range(TILES):
                    left = center[t - 1] if t else before
                    right = center[t + 1] if t < TILES - 1 else after
                    total = (rows[i][t] + center[t]) + (rows[i + 2][t] + (left + right))
                    cut = slice(128 * t, 128 * t + 128)
                    new[r + i, z, cut] = 0.2 * total + source[r + i, z, cut]
        return unused

    lax.fori_loop(0, (WIDE - 2 * number + BLOCK - 1) // BLOCK, block, 0)


def heat_and_sums(
    parts, fields, above, below, pick, order, v0,
    field, out, incoming,
    f0, f1, source, et, cs, ts, square, wsem, esem, osem,
):
    copies = []
    for z in range(ZL):
        copies += [
            pltpu.make_async_copy(fields.at[z], f0.at[HALO : HALO + ROWS, z, :], wsem.at[0, z]),
            pltpu.make_async_copy(above.at[z], f0.at[0:HALO, z, :], wsem.at[1, z]),
            pltpu.make_async_copy(below.at[z], f0.at[HALO + ROWS : WIDE, z, :], wsem.at[2, z]),
        ]
    mode_copies = []
    for m in range(M):
        j = ZL + m
        mode_copies += [
            pltpu.make_async_copy(fields.at[j], et.at[HALO : HALO + ROWS, m, :], esem.at[0, m]),
            pltpu.make_async_copy(above.at[j], et.at[0:HALO, m, :], esem.at[1, m]),
            pltpu.make_async_copy(below.at[j], et.at[HALO + ROWS : WIDE, m, :], esem.at[2, m]),
        ]
    et[:, 8:16, :] = jnp.zeros((WIDE, 8, NY), f32)
    for copy in mode_copies:
        copy.start()
    for copy in copies:
        copy.start()
    real, imag = amplitudes(parts, pick, v0, cs, ts, square, incoming)
    for copy in mode_copies:
        copy.wait()
    heat_load(real, imag, et, source)
    for copy in copies:
        copy.wait()
    place = lax.axis_index("rows")
    first = place == 0
    last = place == lax.axis_size("rows") - 1
    buffers = (f0, f1)
    for number in range(1, PASSES + 1):
        old, new = buffers[(number - 1) % 2], buffers[number % 2]
        one_pass(old, new, source, number)
        if number < PASSES:

            @pl.when(first)
            def _():
                new[HALO - 1] = jnp.zeros((ZL, NY), f32)

            @pl.when(last)
            def _():
                new[HALO + ROWS] = jnp.zeros((ZL, NY), f32)

    done, plain = buffers[PASSES % 2], buffers[1 - PASSES % 2]
    outs = []
    for part in range(ROWS // 8):
        at = slice(8 * part, 8 * part + 8)
        block = done[HALO + 8 * part : HALO + 8 * part + 8].reshape(8 * ZL, NY)
        plain[at] = permuted(block, order, True).reshape(8, ZL, NY)
        for z in range(ZL):
            copy = pltpu.make_async_copy(plain.at[at, z, :], field.at[z, at, :], osem.at[part, z])
            copy.start()
            outs.append(copy)
    acc = sums_of_rows(done, et, HALO, 16)
    packed = packed_sums(acc, square, 1.0 / float(NX * NY), None)
    out[...] = jnp.broadcast_to(packed[None], out.shape)
    for copy in outs:
        copy.wait()


def spread(parts, pick, out):
    total = parts[0]
    for r in range(1, parts.shape[0]):
        total = total + parts[r]
    rows = [total] + [pltpu.roll(total, 128 - 16 * group, 1) for group in range(1, 8)]
    pairs = jnp.concatenate(rows, axis=0)
    table = jnp.dot(pick[...], pairs, precision=highest, preferred_element_type=f32).T
    for m in range(M):
        out[m] = table[0:ZL, M * m : M * m + M]


def shards(segment_warming, eigenfunction_crosssections, segment_phasors, injected_coefficients):
    devices = lax.axis_size("rows")
    hbm = pl.BlockSpec(memory_space=pl.ANY)
    vmem = pl.BlockSpec(memory_space=pltpu.VMEM)
    smem = pl.BlockSpec(memory_space=pltpu.SMEM)
    dma = pltpu.SemaphoreType.DMA
    edge = jax.ShapeDtypeStruct((ZL + M, HALO, NY), f32)
    both = jax.ShapeDtypeStruct((ZL + M, ROWS, NY), f32)
    order = jnp.asarray(lane_order(), dtype=bf16)
    packed = pl.pallas_call(
        start_sums,
        name="start_sums",
        out_shape=jax.ShapeDtypeStruct((devices * GZ, 8, 128), f32),
        in_specs=[hbm, hbm, vmem],
        out_specs=vmem,
        scratch_shapes=[
            pltpu.VMEM((ROWS, ZL, NY), f32),
            pltpu.VMEM((ROWS, 16, NY), f32),
            pltpu.VMEM((128, 128), f32),
            dma((ZL,)),
            dma((M,)),
        ],
        compiler_params=pltpu.CompilerParams(vmem_limit_bytes=16 << 20),
    )(segment_warming, eigenfunction_crosssections, segment_phasors)
    parts = lax.all_to_all(packed, ("rows", "gz"), 0, 0, tiled=True)
    fields, low, high = pl.pallas_call(
        reorder,
        name="reorder",
        out_shape=(both, edge, edge),
        in_specs=[hbm, hbm, vmem, hbm],
        out_specs=(hbm, hbm, hbm),
        scratch_shapes=[
            pltpu.VMEM((ZL + M, ROWS, NY), f32),
            pltpu.VMEM((ZL + M, ROWS, NY), f32),
            dma((2,)),
            dma((4, 3)),
        ],
        cost_estimate=pl.CostEstimate(
            flops=6 * (ZL + M) * ROWS * NY * NY, bytes_accessed=14 << 20, transcendentals=0
        ),
        compiler_params=pltpu.CompilerParams(vmem_limit_bytes=32 << 20),
    )(segment_warming, eigenfunction_crosssections, order, packed)
    forward = [(i, i + 1) for i in range(devices - 1)]
    backward = [(target, origin) for origin, target in forward]
    above = lax.ppermute(low, "rows", forward)
    below = lax.ppermute(high, "rows", backward)
    field, packed, incoming = pl.pallas_call(
        heat_and_sums,
        name="heat_and_sums",
        out_shape=(
            jax.ShapeDtypeStruct((ZL, ROWS, NY), f32),
            jax.ShapeDtypeStruct((devices, 8, 128), f32),
            jax.ShapeDtypeStruct((M, 2, ZL), f32),
        ),
        in_specs=[vmem, hbm, hbm, hbm, vmem, vmem, smem],
        out_specs=(hbm, vmem, vmem),
        scratch_shapes=[
            pltpu.VMEM((TALL, ZL, NY), f32),
            pltpu.VMEM((TALL, ZL, NY), f32),
            pltpu.VMEM((TALL, ZL, NY), f32),
            pltpu.VMEM((WIDE, 16, NY), f32),
            pltpu.VMEM((160, 128), f32),
            pltpu.VMEM((6, 2, 160, 128), f32),
            pltpu.VMEM((128, 128), f32),
            dma((3, ZL)),
            dma((3, M)),
            dma((ROWS // 8, ZL)),
        ],
        compiler_params=pltpu.CompilerParams(vmem_limit_bytes=40 << 20),
    )(
        parts,
        fields,
        above,
        below,
        jnp.asarray(selection(16, 160)),
        order,
        injected_coefficients,
    )
    parts = lax.all_to_all(packed, "rows", 0, 0, tiled=True)
    refreshed = pl.pallas_call(
        spread,
        name="spread",
        out_shape=jax.ShapeDtypeStruct((M, ZL, M), f32),
        in_specs=[vmem, vmem],
        out_specs=vmem,
        compiler_params=pltpu.CompilerParams(vmem_limit_bytes=8 << 20),
    )(parts, jnp.asarray(selection(M, 128)))
    return (field, jnp.transpose(refreshed, (1, 0, 2)), jnp.transpose(incoming, (2, 1, 0)))


def solution(mesh):
    placed = (P("gz", "rows", None), P(None, "rows", None), P("gz", None), P())
    return jax.shard_map(
        shards,
        mesh=mesh,
        in_specs=placed,
        out_specs=(P("gz", "rows", None), P("gz", None, None), P("gz", None, None)),
        check_vma=False,
    )
```

profile of v0, /device:TPU:1, one launch (start us, length us, event | category | flops | bytes accessed | tf_op | source)
XLA Modules:
  0.0 104.8 jit_solution(18074182620999920278)
XLA Ops:
  0.6 0.0 copy-start
  0.6 0.0 copy-start.1
  0.7 1.7 %copy-done.1 = f32[16,32,1024]{2,1,0:T(8,128)S(1)} copy-done((f32[16,32,1024]{2,1,0:T(8,128)S(1)}, f32[16,32,1024]{2,1,0:T(8,128)}, u32[]{:S(2)}) %copy-start.1) | copy-done | bytes 2097176
  2.4 0.0 copy-start.3
  2.4 1.3 %copy-done.3 = f32[10,32,1024]{2,1,0:T(8,128)S(1)} copy-done((f32[10,32,1024]{2,1,0:T(8,128)S(1)}, f32[10,32,1024]{2,1,0:T(8,128)}, u32[]{:S(2)}) %copy-start.3) | copy-done | bytes 1310744
  3.7 0.0 copy-start.7
  3.7 0.7 copy-done.7
  4.4 0.0 copy-start.4
  4.4 5.5 %start_sums.1.unused = f32[128,8,128]{2,1,0:T(8,128)S(1)} custom-call(f32[16,32,1024]{2,1,0:T(8,128)S(1)} %copy-done.1, f32[10,32,1024]{2,1,0:T(8,128)S(1)} %copy-done.3, f32[16,10]{1,0:T(8,128)S(1)} %copy-done.7), custom_call_target="tpu_custom_call" | custom-call | tf_op jit(solution)/shard_map/start_sums/pallas_call | solution.py:428
  9.9 0.0 copy-done
  9.9 0.0 copy-done.4
  9.9 0.0 copy-start.2
  9.9 1.6 %copy-done.2 = f32[16,32,1024]{2,1,0:T(8,128)S(1)} copy-done((f32[16,32,1024]{2,1,0:T(8,128)S(1)}, f32[16,32,1024]{2,1,0:T(8,128)}, u32[]{:S(2)}) %copy-start.2) | copy-done | bytes 2097176
  11.5 0.0 copy-start.5
  11.5 0.0 copy-start.8
  11.5 7.2 %reorder.1 = (f32[26,32,1024]{2,1,0:T(8,128)S(1)}, f32[26,16,1024]{2,1,0:T(8,128)S(1)}, f32[26,16,1024]{2,1,0:T(8,128)S(1)}) custom-call(f32[16,32,1024]{2,1,0:T(8,128)S(1)} %copy-done.2, f32[10,32,1024]{2,1,0:T(8,128)S(1)} %copy-done.4, bf16[1024,1024]{1,0:T(8,128)(2,1)S(1)} %copy-done, f32[128,8,128]{2,1,0:T(8,128)S(1)} %start_sums.1.unused), custom_call_target="tpu_custom_call" | custom-call | flops 5234491392 | bytes 14680064 | tf_op jit(solution)/shard_map/reorder/pallas_call | solution.py:444
  18.7 4.5 %collective-permute-start = (f32[26,16,1024]{2,1,0:T(8,128)S(1)}, f32[26,16,1024]{2,1,0:T(8,128)S(1)}, u32[]{:S(2)}, u32[]{:S(2)}) collective-permute-start(f32[26,16,1024]{2,1,0:T(8,128)S(1)} %get-tuple-element.10), channel_id=1, source_target_pairs={{0,4},{4,8},{8,12},{12,16},{16,20},{20,24},{24,28},{28,32},{32,36}... | collective-permute-start | bytes 5111816 | tf_op jit(solution)/shard_map/ppermute | solution.py:463
  23.2 1.9 %collective-permute-start.1 = (f32[26,16,1024]{2,1,0:T(8,128)S(1)}, f32[26,16,1024]{2,1,0:T(8,128)S(1)}, u32[]{:S(2)}, u32[]{:S(2)}) collective-permute-start(f32[26,16,1024]{2,1,0:T(8,128)S(1)} %get-tuple-element.11), channel_id=1, source_target_pairs={{4,0},{8,4},{12,8},{16,12},{20,16},{24,20},{28,24},{32,28},{36,32}... | collective-permute-start | bytes 5111816 | tf_op jit(solution)/shard_map/ppermute | solution.py:464
  25.1 32.0 %all_to_all.10.parts = f32[128,8,128]{2,1,0:T(8,128)S(1)} all-to-all(f32[128,8,128]{2,1,0:T(8,128)S(1)} %start_sums.1.unused), channel_id=1, replica_groups=mesh['rows'=32,'gz'=4] {'rows','gz'}, dimensions={0} | all-to-all | bytes 1048576 | tf_op jit(solution)/shard_map/all_to_all | solution.py:443
  57.1 0.0 collective-permute-done.above
  57.1 0.0 collective-permute-done.1.below
  57.1 0.0 copy-done.5
  57.1 0.0 copy-done.8
  57.1 0.0 copy-start.6
  57.2 31.4 %heat_and_sums.1 = (f32[16,32,1024]{2,1,0:T(8,128)}, f32[32,8,128]{2,1,0:T(8,128)S(1)}, f32[10,2,16]{2,1,0:T(2,128)}) custom-call(f32[128,8,128]{2,1,0:T(8,128)S(1)} %all_to_all.10.parts, f32[26,32,1024]{2,1,0:T(8,128)S(1)} %get-tuple-element.9.fields, f32[26,16,1024]{2,1,0:T(8,128)S(1)} %collective-permute-done.above, ...), custom_call_target="tpu_custom_call" | custom-call | tf_op jit(solution)/shard_map/heat_and_sums/pallas_call | solution.py:465
  88.6 15.2 %all_to_all.11.parts = f32[32,8,128]{2,1,0:T(8,128)S(1)} all-to-all(f32[32,8,128]{2,1,0:T(8,128)S(1)} %get-tuple-element.13), channel_id=1, replica_groups=mesh['rows'=32,'gz'=4] {'rows'}, dimensions={0} | all-to-all | bytes 262144 | tf_op jit(solution)/shard_map/all_to_all | solution.py:497
  103.7 0.0 copy-done.6
  103.7 1.1 %spread.1 = f32[10,16,10]{2,1,0:T(8,128)} custom-call(f32[32,8,128]{2,1,0:T(8,128)S(1)} %all_to_all.11.parts, f32[128,64]{1,0:T(8,128)S(1)} %copy-done.6), custom_call_target="tpu_custom_call" | custom-call | tf_op jit(solution)/shard_map/spread/pallas_call | solution.py:498
Async XLA Ops:
  0.6 9.3 %copy-start = (bf16[1024,1024]{1,0:T(8,128)(2,1)S(1)}, bf16[1024,1024]{1,0:T(8,128)(2,1)}, u32[]{:S(2)}) copy-start(bf16[1024,1024]{1,0:T(8,128)(2,1)} %constant.6.clone.order) | copy-start | bytes 6291460
  0.6 1.7 %copy-start.1 = (f32[16,32,1024]{2,1,0:T(8,128)S(1)}, f32[16,32,1024]{2,1,0:T(8,128)}, u32[]{:S(2)}) copy-start(f32[16,32,1024]{2,1,0:T(8,128)} %w.3) | copy-start | bytes 6291460
  2.4 1.3 %copy-start.3 = (f32[10,32,1024]{2,1,0:T(8,128)S(1)}, f32[10,32,1024]{2,1,0:T(8,128)}, u32[]{:S(2)}) copy-start(f32[10,32,1024]{2,1,0:T(8,128)} %e.3) | copy-start | bytes 3932164
  3.7 0.7 copy-start.7
  4.4 5.5 %copy-start.4 = (f32[10,32,1024]{2,1,0:T(8,128)S(1)}, f32[10,32,1024]{2,1,0:T(8,128)}, u32[]{:S(2)}) copy-start(f32[10,32,1024]{2,1,0:T(8,128)} %e.3) | copy-start | bytes 3932164
  9.9 1.6 %copy-start.2 = (f32[16,32,1024]{2,1,0:T(8,128)S(1)}, f32[16,32,1024]{2,1,0:T(8,128)}, u32[]{:S(2)}) copy-start(f32[16,32,1024]{2,1,0:T(8,128)} %w.3) | copy-start | bytes 6291460
  11.5 45.6 %copy-start.5 = (f32[160,64]{1,0:T(8,128)S(1)}, f32[160,64]{1,0:T(8,128)}, u32[]{:S(2)}) copy-start(f32[160,64]{1,0:T(8,128)} %constant.7.clone.pick) | copy-start | bytes 122884
  11.5 45.6 %copy-start.8 = (f32[2,10]{1,0:T(2,128)S(1)}, f32[2,10]{1,0:T(2,128)}, u32[]{:S(2)}) copy-start(f32[2,10]{1,0:T(2,128)} %v0.1) | copy-start | bytes 244
  18.7 38.4 %collective-permute-start = (f32[26,16,1024]{2,1,0:T(8,128)S(1)}, f32[26,16,1024]{2,1,0:T(8,128)S(1)}, u32[]{:S(2)}, u32[]{:S(2)}) collective-permute-start(f32[26,16,1024]{2,1,0:T(8,128)S(1)} %get-tuple-element.10), channel_id=1, source_target_pairs={{0,4},{4,8},{8,12},{12,16},{16,20},{20,24},{24,28},{28,32},{32,36}... | collective-permute-start | bytes 5111816 | tf_op jit(solution)/shard_map/ppermute | solution.py:463
  23.2 33.9 %collective-permute-start.1 = (f32[26,16,1024]{2,1,0:T(8,128)S(1)}, f32[26,16,1024]{2,1,0:T(8,128)S(1)}, u32[]{:S(2)}, u32[]{:S(2)}) collective-permute-start(f32[26,16,1024]{2,1,0:T(8,128)S(1)} %get-tuple-element.11), channel_id=1, source_target_pairs={{4,0},{8,4},{12,8},{16,12},{20,16},{24,20},{28,24},{32,28},{36,32}... | collective-permute-start | bytes 5111816 | tf_op jit(solution)/shard_map/ppermute | solution.py:464
  57.1 46.6 %copy-start.6 = (f32[128,64]{1,0:T(8,128)S(1)}, f32[128,64]{1,0:T(8,128)}, u32[]{:S(2)}) copy-start(f32[128,64]{1,0:T(8,128)} %constant.8.clone.pick) | copy-start | bytes 98308
where the time goes:
time: 105 us
  blocking collectives  47.2 us (45%)
  Pallas kernels  45.1 us (43%)
  starting transfers between devices  6.42 us (6%)
  local copies, waits for them, and re-layouts  5.36 us (5%)
    all_to_all x1, blocking collectives, shards(): parts = lax.all_to_all(packed, ('rows', 'gz'), 0, 0, tiled=True)  32 us
    pallas_call x1, Pallas kernels, shards(): pl.pallas_call(heat_and_sums, name='heat_and_sums', out_shape=(jax.ShapeD...  31.4 us
    all_to_all x1, blocking collectives, shards(): parts = lax.all_to_all(packed, 'rows', 0, 0, tiled=True)  15.2 us
    pallas_call x1, Pallas kernels, shards(): pl.pallas_call(reorder, name='reorder', out_shape=(both, edge, edge), in_...  7.16 us
    pallas_call x1, Pallas kernels, shards(): pl.pallas_call(start_sums, name='start_sums', out_shape=jax.ShapeDtypeStr...  5.49 us
    unnamed x18, local copies, waits for them, and re-layouts  5.36 us
    ppermute x1, starting transfers between devices, shards(): above = lax.ppermute(low, 'rows', forward)  4.5 us
  transfers between devices with their start and end apart: 2, of which 0 were waited for; matrix products, arithmetic and copies ran while one was open for 0% of the time, Pallas kernels for 0%

commit v1 on v0

--- a/solution.py
+++ b/solution.py
@@ -86,15 +86,15 @@
     return jnp.concatenate(groups, axis=0)
 
 
-def sums_of_rows(field_ref, modes_ref, first, unroll):
+def sums_of_rows(field_ref, first, modes_ref, modes_first, count, unroll, start):
     def step(r, acc):
-        products = jnp.concatenate(split(pair_products(modes_ref, first + r)), axis=0)
+        products = jnp.concatenate(split(pair_products(modes_ref, modes_first + r)), axis=0)
         warmth = jnp.concatenate(split(field_ref[first + r]), axis=0)
         return acc + lax.dot_general(
             products, warmth, (((1,), (1,)), ((), ())), preferred_element_type=f32
         )
 
-    return lax.fori_loop(0, ROWS, step, jnp.zeros((128, 32), f32), unroll=unroll)
+    return lax.fori_loop(0, count, step, start, unroll=unroll)
 
 
 def packed_sums(acc, pad_ref, scale, extra):
@@ -112,14 +112,30 @@
     return packed
 
 
-def start_sums(w, e, ph, out, wt, et, pad, wsem, esem):
-    copies = []
-    for z in range(ZL):
-        copies.append(pltpu.make_async_copy(w.at[z], wt.at[:, z, :], wsem.at[z]))
-    for m in range(M):
-        copies.append(pltpu.make_async_copy(e.at[m], et.at[:, m, :], esem.at[m]))
-    for copy in copies:
-        copy.start()
+def start_sums(w, e, ph, out, low, high, wt, et, pad, wsem, esem, hsem):
+    half = ROWS // 2
+    chunks, edges = [], []
+    for part, edge in enumerate((high, low)):
+        at = slice(half * part, half * (part + 1))
+        chunks.append(
+            [
+                pltpu.make_async_copy(e.at[m, at, :], et.at[at, m, :], esem.at[part, m])
+                for m in range(M)
+            ]
+            + [
+                pltpu.make_async_copy(w.at[z, at, :], wt.at[at, z, :], wsem.at[part, z])
+                for z in range(ZL)
+            ]
+        )
+        edges += [
+            pltpu.make_async_copy(wt.at[at, z, :], edge.at[z], hsem.at[part, z]) for z in range(ZL)
+        ] + [
+            pltpu.make_async_copy(et.at[at, m, :], edge.at[ZL + m], hsem.at[part, ZL + m])
+            for m in range(M)
+        ]
+    for copies in chunks:
+        for copy in copies:
+            copy.start()
     pad[...] = jnp.zeros((128, 128), f32)
     pad[0:ZL, 0:M] = ph[...]
     turned = pad[...].T
@@ -130,63 +146,64 @@
             row == place, jnp.broadcast_to(turned[m : m + 1, :], (64, 128)), 0.0
         )
     phases = phases * jnp.where(lax.axis_index("rows") == 0, 1.0, 0.0)
-    for copy in copies:
-        copy.wait()
-    acc = sums_of_rows(wt, et, 0, 16)
+    acc = jnp.zeros((128, 32), f32)
+    for part, copies in enumerate(chunks):
+        for copy in copies:
+            copy.wait()
+        for copy in edges[(ZL + M) * part : (ZL + M) * (part + 1)]:
+            copy.start()
+        acc = sums_of_rows(wt, half * part, et, half * part, half, 16, acc)
     packed = packed_sums(acc, pad, 2.0 / float(NX * NY), phases)
     out[...] = jnp.broadcast_to(packed[None], out.shape)
-
-
-def three_parts(value):
-    first = value.astype(bf16)
-    rest = value - first.astype(f32)
-    second = rest.astype(bf16)
-    third = (rest - second.astype(f32)).astype(bf16)
-    return jnp.concatenate([first, second, third], axis=0)
-
-
-def lane_order():
-    column = np.arange(NY)
-    order = np.zeros((NY, NY), np.float32)
-    order[column, (column % TILES) * 128 + column // TILES] = 1.0
-    return order
-
-
-def permuted(value, order_ref, back):
-    count = value.shape[0]
-    moved = lax.dot_general(
-        three_parts(value),
-        order_ref[...],
-        (((1,), (1 if back else 0,)), ((), ())),
-        preferred_element_type=f32,
+    for copy in edges:
+        copy.wait()
+
+
+def spots(k):
+    return pl.ds(64 * (k % 2) + k // 2, 8, stride=8)
+
+
+def turn_in(value, new, row):
+    stacked = jnp.concatenate([value[:, 128 * t : 128 * t + 128] for t in range(TILES)], axis=0)
+    across = stacked.T
+    for k in range(16):
+        new[row, spots(k), :] = across[8 * k : 8 * k + 8]
+
+
+def turn_out(old, row, new, new_row):
+    across = jnp.concatenate([old[row, spots(k), :] for k in range(16)], axis=0).T
+    for t in range(TILES):
+        new[new_row, :, 128 * t : 128 * t + 128] = across[16 * t : 16 * t + 16]
+
+
+def turn_warming(w, above, below, unused, out, raw, new, lsem, ssem):
+    sides = (
+        (w, HALO, ROWS),
+        (above, 0, HALO),
+        (below, HALO + ROWS, HALO),
     )
-    return (moved[0:count] + moved[count : 2 * count]) + moved[2 * count :]
-
-
-def reorder(w, e, order, unused, full, low, high, raw, moved, lsem, ssem):
-    loads = [
-        pltpu.make_async_copy(w, raw.at[0:ZL], lsem.at[0]),
-        pltpu.make_async_copy(e, raw.at[ZL : ZL + M], lsem.at[1]),
-    ]
-    for copy in loads:
-        copy.start()
-    for copy in loads:
-        copy.wait()
-    stores = []
-    for part, (start, stop) in enumerate(((0, 8), (8, 16), (16, 21), (21, 26))):
-        rows = (stop - start) * ROWS
-        block = raw[start:stop].reshape(rows, NY)
-        moved[start:stop] = permuted(block, order, False).reshape(stop - start, ROWS, NY)
-        here = slice(start, stop)
-        stores += [
-            pltpu.make_async_copy(
-                moved.at[here, ROWS - HALO : ROWS, :], low.at[here], ssem.at[part, 0]
-            ),
-            pltpu.make_async_copy(moved.at[here, 0:HALO, :], high.at[here], ssem.at[part, 1]),
-            pltpu.make_async_copy(moved.at[here], full.at[here], ssem.at[part, 2]),
-        ]
-        for copy in stores[-3:]:
+    loads, stores = [], []
+    for side, (origin, start, count) in enumerate(sides):
+        at = slice(start, start + count)
+        loads.append(
+            [
+                pltpu.make_async_copy(origin.at[z], raw.at[at, z, :], lsem.at[side, z])
+                for z in range(ZL)
+            ]
+        )
+        stores.append(pltpu.make_async_copy(new.at[at], out.at[at], ssem.at[side]))
+        for copy in loads[side]:
             copy.start()
+    for side, (origin, start, count) in enumerate(sides):
+        for copy in loads[side]:
+            copy.wait()
+
+        def step(r, unused):
+            turn_in(raw[start + r], new, start + r)
+            return unused
+
+        lax.fori_loop(0, count, step, 0, unroll=8)
+        stores[side].start()
     for copy in stores:
         copy.wait()
 
@@ -306,7 +323,7 @@
         stacked = jnp.concatenate([high_e, low_e, high_e, low_e], axis=0)
         field = jnp.dot(weights, stacked, preferred_element_type=f32)
         re, im = field[0:16], field[16:32]
-        source_ref[r] = 0.01 * (re * re + im * im)
+        turn_in(0.01 * (re * re + im * im), source_ref, r)
         return unused
 
     lax.fori_loop(0, WIDE, step, 0, unroll=16)
@@ -314,63 +331,64 @@
 
 def one_pass(old, new, source, number):
     lane = lax.broadcasted_iota(jnp.int32, (8, 128), 1)
-    first_lane = lane == 0
-    last_lane = lane == 127
+    sub = lax.broadcasted_iota(jnp.int32, (8, 128), 0)
 
     def block(b, unused):
         r = number + BLOCK * b
         for half in range(2):
-            z = slice(8 * half, 8 * half + 8)
-            rows = [
-                [old[r - 1 + i, z, 128 * t : 128 * t + 128] for t in range(TILES)]
-                for i in range(BLOCK + 2)
-            ]
+            some = range(8 * half, 8 * half + 8)
+
+            def register(row, v):
+                return old[row, 8 * v : 8 * v + 8, :]
+
+            rows = [{v: register(r - 1 + i, v) for v in some} for i in range(BLOCK + 2)]
             for i in range(BLOCK):
-                center = rows[i + 1]
-                before = jnp.where(first_lane, 0.0, pltpu.roll(center[TILES - 1], 1, 1))
-                after = jnp.where(last_lane, 0.0, pltpu.roll(center[0], 127, 1))
-                for t in range(TILES):
-                    left = center[t - 1] if t else before
-                    right = center[t + 1] if t < TILES - 1 else after
-                    total = (rows[i][t] + center[t]) + (rows[i + 2][t] + (left + right))
-                    cut = slice(128 * t, 128 * t + 128)
-                    new[r + i, z, cut] = 0.2 * total + source[r + i, z, cut]
+                center = dict(rows[i + 1])
+                if half == 0:
+                    near = pltpu.roll(register(r + i, 15), 1, 0)
+                    far = jnp.where(lane < 16, 0.0, pltpu.roll(near, 16, 1))
+                    center[-1] = jnp.where(sub == 0, far, near)
+                    center[8] = register(r + i, 8)
+                else:
+                    near = pltpu.roll(register(r + i, 0), 7, 0)
+                    far = jnp.where(lane >= 112, 0.0, pltpu.roll(near, 112, 1))
+                    center[16] = jnp.where(sub == 7, far, near)
+                    center[7] = register(r + i, 7)
+                for v in some:
+                    sides = center[v - 1] + center[v + 1]
+                    total = (rows[i][v] + center[v]) + (rows[i + 2][v] + sides)
+                    cut = slice(8 * v, 8 * v + 8)
+                    new[r + i, cut, :] = 0.2 * total + source[r + i, cut, :]
         return unused
 
     lax.fori_loop(0, (WIDE - 2 * number + BLOCK - 1) // BLOCK, block, 0)
 
 
 def heat_and_sums(
-    parts, fields, above, below, pick, order, v0,
+    parts, warm, e, edge_above, edge_below, pick, v0,
     field, out, incoming,
-    f0, f1, source, et, cs, ts, square, wsem, esem, osem,
+    f0, f1, source, et, plain, cs, ts, square, wsem, esem, osem,
 ):
-    copies = []
-    for z in range(ZL):
-        copies += [
-            pltpu.make_async_copy(fields.at[z], f0.at[HALO : HALO + ROWS, z, :], wsem.at[0, z]),
-            pltpu.make_async_copy(above.at[z], f0.at[0:HALO, z, :], wsem.at[1, z]),
-            pltpu.make_async_copy(below.at[z], f0.at[HALO + ROWS : WIDE, z, :], wsem.at[2, z]),
-        ]
+    warm_copy = pltpu.make_async_copy(warm, f0.at[0:WIDE], wsem)
     mode_copies = []
     for m in range(M):
-        j = ZL + m
-        mode_copies += [
-            pltpu.make_async_copy(fields.at[j], et.at[HALO : HALO + ROWS, m, :], esem.at[0, m]),
-            pltpu.make_async_copy(above.at[j], et.at[0:HALO, m, :], esem.at[1, m]),
-            pltpu.make_async_copy(below.at[j], et.at[HALO + ROWS : WIDE, m, :], esem.at[2, m]),
-        ]
+        for side, (origin, at) in enumerate(
+            (
+                (e.at[m], slice(HALO, HALO + ROWS)),
+                (edge_above.at[ZL + m], slice(0, HALO)),
+                (edge_below.at[ZL + m], slice(HALO + ROWS, WIDE)),
+            )
+        ):
+            mode_copies.append(pltpu.make_async_copy(origin, et.at[at, m, :], esem.at[side, m]))
     et[:, 8:16, :] = jnp.zeros((WIDE, 8, NY), f32)
     for copy in mode_copies:
         copy.start()
-    for copy in copies:
-        copy.start()
+    warm_copy.start()
     real, imag = amplitudes(parts, pick, v0, cs, ts, square, incoming)
     for copy in mode_copies:
         copy.wait()
     heat_load(real, imag, et, source)
-    for copy in copies:
-        copy.wait()
+    warm_copy.wait()
     place = lax.axis_index("rows")
     first = place == 0
     last = place == lax.axis_size("rows") - 1
@@ -382,23 +400,23 @@
 
             @pl.when(first)
             def _():
-                new[HALO - 1] = jnp.zeros((ZL, NY), f32)
+                new[HALO - 1] = jnp.zeros((128, 128), f32)
 
             @pl.when(last)
             def _():
-                new[HALO + ROWS] = jnp.zeros((ZL, NY), f32)
-
-    done, plain = buffers[PASSES % 2], buffers[1 - PASSES % 2]
+                new[HALO + ROWS] = jnp.zeros((128, 128), f32)
+
+    done = buffers[PASSES % 2]
     outs = []
     for part in range(ROWS // 8):
         at = slice(8 * part, 8 * part + 8)
-        block = done[HALO + 8 * part : HALO + 8 * part + 8].reshape(8 * ZL, NY)
-        plain[at] = permuted(block, order, True).reshape(8, ZL, NY)
+        for r in range(8 * part, 8 * part + 8):
+            turn_out(done, HALO + r, plain, r)
         for z in range(ZL):
             copy = pltpu.make_async_copy(plain.at[at, z, :], field.at[z, at, :], osem.at[part, z])
             copy.start()
             outs.append(copy)
-    acc = sums_of_rows(done, et, HALO, 16)
+    acc = sums_of_rows(plain, 0, et, HALO, ROWS, 16, jnp.zeros((128, 32), f32))
     packed = packed_sums(acc, square, 1.0 / float(NX * NY), None)
     out[...] = jnp.broadcast_to(packed[None], out.shape)
     for copy in outs:
@@ -416,52 +434,55 @@
         out[m] = table[0:ZL, M * m : M * m + M]
 
 
+def on_hbm(array):
+    return pltpu.with_memory_space_constraint(array, pltpu.HBM)
+
+
 def shards(segment_warming, eigenfunction_crosssections, segment_phasors, injected_coefficients):
     devices = lax.axis_size("rows")
-    hbm = pl.BlockSpec(memory_space=pl.ANY)
+    hbm = pl.BlockSpec(memory_space=pltpu.HBM)
     vmem = pl.BlockSpec(memory_space=pltpu.VMEM)
     smem = pl.BlockSpec(memory_space=pltpu.SMEM)
     dma = pltpu.SemaphoreType.DMA
-    edge = jax.ShapeDtypeStruct((ZL + M, HALO, NY), f32)
-    both = jax.ShapeDtypeStruct((ZL + M, ROWS, NY), f32)
-    order = jnp.asarray(lane_order(), dtype=bf16)
-    packed = pl.pallas_call(
+    edge = pltpu.HBM((ZL + M, HALO, NY), f32)
+    slab_vmem = pltpu.VMEM((ROWS, 16, NY), f32)
+    warming, shapes = on_hbm(segment_warming), on_hbm(eigenfunction_crosssections)
+    packed, low, high = pl.pallas_call(
         start_sums,
         name="start_sums",
-        out_shape=jax.ShapeDtypeStruct((devices * GZ, 8, 128), f32),
+        out_shape=(jax.ShapeDtypeStruct((devices * GZ, 8, 128), f32), edge, edge),
         in_specs=[hbm, hbm, vmem],
-        out_specs=vmem,
+        out_specs=(vmem, hbm, hbm),
         scratch_shapes=[
-            pltpu.VMEM((ROWS, ZL, NY), f32),
-            pltpu.VMEM((ROWS, 16, NY), f32),
+            slab_vmem,
+            slab_vmem,
             pltpu.VMEM((128, 128), f32),
-            dma((ZL,)),
-            dma((M,)),
+            dma((2, ZL)),
+            dma((2, M)),
+            dma((2, ZL + M)),
         ],
         compiler_params=pltpu.CompilerParams(vmem_limit_bytes=16 << 20),
-    )(segment_warming, eigenfunction_crosssections, segment_phasors)
-    parts = lax.all_to_all(packed, ("rows", "gz"), 0, 0, tiled=True)
-    fields, low, high = pl.pallas_call(
-        reorder,
-        name="reorder",
-        out_shape=(both, edge, edge),
-        in_specs=[hbm, hbm, vmem, hbm],
-        out_specs=(hbm, hbm, hbm),
-        scratch_shapes=[
-            pltpu.VMEM((ZL + M, ROWS, NY), f32),
-            pltpu.VMEM((ZL + M, ROWS, NY), f32),
-            dma((2,)),
-            dma((4, 3)),
-        ],
-        cost_estimate=pl.CostEstimate(
-            flops=6 * (ZL + M) * ROWS * NY * NY, bytes_accessed=14 << 20, transcendentals=0
-        ),
-        compiler_params=pltpu.CompilerParams(vmem_limit_bytes=32 << 20),
-    )(segment_warming, eigenfunction_crosssections, order, packed)
+    )(warming, shapes, segment_phasors)
     forward = [(i, i + 1) for i in range(devices - 1)]
     backward = [(target, origin) for origin, target in forward]
     above = lax.ppermute(low, "rows", forward)
     below = lax.ppermute(high, "rows", backward)
+    parts = lax.all_to_all(packed, ("rows", "gz"), 0, 0, tiled=True)
+    warm = pl.pallas_call(
+        turn_warming,
+        name="turn_warming",
+        out_shape=pltpu.HBM((WIDE, 128, 128), f32),
+        in_specs=[hbm, hbm, hbm, pl.BlockSpec(memory_space=pl.ANY)],
+        out_specs=hbm,
+        scratch_shapes=[
+            pltpu.VMEM((WIDE, ZL, NY), f32),
+            pltpu.VMEM((WIDE, 128, 128), f32),
+            dma((3, ZL)),
+            dma((3,)),
+        ],
+        compiler_params=pltpu.CompilerParams(vmem_limit_bytes=16 << 20),
+    )(warming, on_hbm(above), on_hbm(below), packed)
+    wide_vmem = pltpu.VMEM((TALL, 128, 128), f32)
     field, packed, incoming = pl.pallas_call(
         heat_and_sums,
         name="heat_and_sums",
@@ -470,28 +491,29 @@
             jax.ShapeDtypeStruct((devices, 8, 128), f32),
             jax.ShapeDtypeStruct((M, 2, ZL), f32),
         ),
-        in_specs=[vmem, hbm, hbm, hbm, vmem, vmem, smem],
+        in_specs=[vmem, hbm, hbm, hbm, hbm, vmem, smem],
         out_specs=(hbm, vmem, vmem),
         scratch_shapes=[
-            pltpu.VMEM((TALL, ZL, NY), f32),
-            pltpu.VMEM((TALL, ZL, NY), f32),
-            pltpu.VMEM((TALL, ZL, NY), f32),
+            wide_vmem,
+            wide_vmem,
+            wide_vmem,
             pltpu.VMEM((WIDE, 16, NY), f32),
+            slab_vmem,
             pltpu.VMEM((160, 128), f32),
             pltpu.VMEM((6, 2, 160, 128), f32),
             pltpu.VMEM((128, 128), f32),
-            dma((3, ZL)),
+            dma,
             dma((3, M)),
             dma((ROWS // 8, ZL)),
         ],
         compiler_params=pltpu.CompilerParams(vmem_limit_bytes=40 << 20),
     )(
         parts,
-        fields,
-        above,
-        below,
+        on_hbm(warm),
+        shapes,
+        on_hbm(above),
+        on_hbm(below),
         jnp.asarray(selection(16, 160)),
-        order,
         injected_coefficients,
     )
     parts = lax.all_to_all(packed, "rows", 0, 0, tiled=True)

time: 105 us -> 88.1 us (0.84)
  blocking collectives: 47.2 us -> 15.2 us
  waiting for transfers between devices: 0.01 us -> 16.7 us
  starting transfers between devices: 6.42 us -> 17.1 us
  Pallas kernels: 45.1 us -> 37.4 us
  local copies, waits for them, and re-layouts: 5.36 us -> 0.71 us
    all_to_all x1 -> x0, blocking collectives: 32 us -> none  [shards(): parts = lax.all_to_all(packed, ('rows', 'gz'), 0, 0, tiled=True)]
    all_to_all x0 -> x1, starting transfers between devices: none -> 10.6 us  [shards(): parts = lax.all_to_all(packed, ('rows', 'gz'), 0, 0, tiled=True)]
    ppermute x1, waiting for transfers between devices: 0.01 us -> 9.27 us  [shards(): above = lax.ppermute(low, 'rows', forward)]
    pallas_call x1, Pallas kernels: 31.4 us -> 23.3 us  [shards(): pl.pallas_call(heat_and_sums, name='heat_and_sums', out_shape=(jax.ShapeD...]
    unnamed x18 -> x10, local copies, waits for them, and re-layouts: 5.36 us -> 0.71 us
    ppermute x1, waiting for transfers between devices: 0.01 us -> 4.58 us  [shards(): below = lax.ppermute(high, 'rows', backward)]
    all_to_all x0 -> x1, waiting for transfers between devices: none -> 2.8 us  [shards(): parts = lax.all_to_all(packed, ('rows', 'gz'), 0, 0, tiled=True)]
  transfers between devices with their start and end apart: 2 -> 3, of which waited for: 0 -> 3; matrix products, arithmetic and copies ran while one was open for 0% -> 0% of each run, Pallas kernels for 0% -> 6%
where the time goes in v1:
time: 88.1 us; the launch traced here: 87.8 us
  Pallas kernels  37.4 us (42%)
  starting transfers between devices  17.1 us (19%)
  waiting for transfers between devices  16.7 us (19%)
  blocking collectives  15.2 us (17%)
    pallas_call x1, Pallas kernels, shards(): pl.pallas_call(heat_and_sums, name='heat_and_sums', out_shape=(jax.ShapeD...  23.3 us
    all_to_all x1, blocking collectives, shards(): parts = lax.all_to_all(packed, 'rows', 0, 0, tiled=True)  15.2 us
    all_to_all x1, starting transfers between devices, shards(): parts = lax.all_to_all(packed, ('rows', 'gz'), 0, 0, tiled=True)  10.6 us
    ppermute x1, waiting for transfers between devices, shards(): above = lax.ppermute(low, 'rows', forward)  9.27 us
    pallas_call x1, Pallas kernels, shards(): pl.pallas_call(start_sums, name='start_sums', out_shape=(jax.ShapeDtypeSt...  8.26 us
    pallas_call x1, Pallas kernels, shards(): pl.pallas_call(turn_warming, name='turn_warming', out_shape=pltpu.HBM((WI...  4.85 us
    ppermute x1, waiting for transfers between devices, shards(): below = lax.ppermute(high, 'rows', backward)  4.58 us
    ppermute x1, starting transfers between devices, shards(): above = lax.ppermute(low, 'rows', forward)  4.5 us
  transfers between devices with their start and end apart: 3, of which 3 were waited for; matrix products, arithmetic and copies ran while one was open for 0% of the time, Pallas kernels for 6%

profile of v1, /device:TPU:1, one launch (start us, length us, event | category | flops | bytes accessed | tf_op | source)
XLA Modules:
  0.0 87.8 jit_solution(11458754899705269921)
XLA Ops:
  0.6 0.0 copy-start.2
  0.6 0.7 copy-done.2
  1.3 8.3 %start_sums.1 = (f32[128,8,128]{2,1,0:T(8,128)}, f32[26,16,1024]{2,1,0:T(8,128)}, f32[26,16,1024]{2,1,0:T(8,128)}) custom-call(f32[16,32,1024]{2,1,0:T(8,128)} %w.3, f32[10,32,1024]{2,1,0:T(8,128)} %e.3, f32[16,10]{1,0:T(8,128)S(1)} %copy-done.2), custom_call_target="tpu_custom_call" | custom-call | tf_op jit(solution)/shard_map/start_sums/pallas_call | solution.py:450
  9.6 4.5 %collective-permute-start = (f32[26,16,1024]{2,1,0:T(8,128)}, f32[26,16,1024]{2,1,0:T(8,128)S(1)}, u32[]{:S(2)}, u32[]{:S(2)}) collective-permute-start(f32[26,16,1024]{2,1,0:T(8,128)} %get-tuple-element.10), channel_id=1, source_target_pairs={{0,4},{4,8},{8,12},{12,16},{16,20},{20,24},{24,28},{28,32},{32,36}... | collective-permute-start | bytes 5111816 | tf_op jit(solution)/shard_map/ppermute | solution.py:468
  14.1 1.9 %collective-permute-start.1 = (f32[26,16,1024]{2,1,0:T(8,128)}, f32[26,16,1024]{2,1,0:T(8,128)}, u32[]{:S(2)}, u32[]{:S(2)}) collective-permute-start(f32[26,16,1024]{2,1,0:T(8,128)} %get-tuple-element.11), channel_id=1, source_target_pairs={{4,0},{8,4},{12,8},{16,12},{20,16},{24,20},{28,24},{32,28},{36,32}... | collective-permute-start | bytes 5111816 | tf_op jit(solution)/shard_map/ppermute | solution.py:469
  16.0 10.6 %all-to-all-start = ((f32[128,8,128]{2,1,0:T(8,128)}), f32[128,8,128]{2,1,0:T(8,128)S(1)}, u32[]{:S(2)}, u32[]{:S(2)}) async-start(f32[128,8,128]{2,1,0:T(8,128)} %get-tuple-element.9.unused), calls=%async_computation | async-start | bytes 1048576 | tf_op jit(solution)/shard_map/all_to_all | solution.py:470
  26.7 0.0 copy-start
  26.7 0.0 copy-start.3
  26.7 9.3 %collective-permute-done.above.edge_above = f32[26,16,1024]{2,1,0:T(8,128)S(1)} collective-permute-done((f32[26,16,1024]{2,1,0:T(8,128)}, f32[26,16,1024]{2,1,0:T(8,128)S(1)}, u32[]{:S(2)}, u32[]{:S(2)}) %collective-permute-start) | collective-permute-done | bytes 1703968 | tf_op jit(solution)/shard_map/ppermute | solution.py:468
  36.0 0.0 copy-start.4
  36.0 4.6 %collective-permute-done.1.below.edge_below = f32[26,16,1024]{2,1,0:T(8,128)} collective-permute-done((f32[26,16,1024]{2,1,0:T(8,128)}, f32[26,16,1024]{2,1,0:T(8,128)}, u32[]{:S(2)}, u32[]{:S(2)}) %collective-permute-start.1) | collective-permute-done | bytes 1703968 | tf_op jit(solution)/shard_map/ppermute | solution.py:469
  40.6 0.0 copy-done.4
  40.6 4.9 %turn_warming.1.warm = f32[64,128,128]{2,1,0:T(8,128)} custom-call(f32[16,32,1024]{2,1,0:T(8,128)} %w.3, f32[26,16,1024]{2,1,0:T(8,128)} %copy-done.4, f32[26,16,1024]{2,1,0:T(8,128)} %collective-permute-done.1.below.edge_below, f32[128,8,128]{2,1,0:T(8,128)} %get-tuple-element.9.unused), custom_call_target="tpu_custom_call" | custom-call | tf_op jit(solution)/shard_map/turn_warming/pallas_call | solution.py:471
  45.4 0.0 copy-start.1
  45.4 2.8 %all-to-all-done.parts = f32[128,8,128]{2,1,0:T(8,128)S(1)} async-done(((f32[128,8,128]{2,1,0:T(8,128)}), f32[128,8,128]{2,1,0:T(8,128)S(1)}, u32[]{:S(2)}, u32[]{:S(2)}) %all-to-all-start) | async-done | bytes 524320 | tf_op jit(solution)/shard_map/all_to_all | solution.py:470
  48.2 0.0 copy-done
  48.2 0.0 copy-done.3
  48.2 23.3 %heat_and_sums.1 = (f32[16,32,1024]{2,1,0:T(8,128)}, f32[32,8,128]{2,1,0:T(8,128)S(1)}, f32[10,2,16]{2,1,0:T(2,128)}) custom-call(f32[128,8,128]{2,1,0:T(8,128)S(1)} %all-to-all-done.parts, f32[64,128,128]{2,1,0:T(8,128)} %turn_warming.1.warm, f32[10,32,1024]{2,1,0:T(8,128)} %e.3, f32[26,16,1024]{2,1,0:T(8,128)} %copy-done.4, ...), custom_call_target="tpu_custom_call" | custom-call | tf_op jit(solution)/shard_map/heat_and_sums/pallas_call | solution.py:486
  71.5 15.2 %all_to_all.10.parts = f32[32,8,128]{2,1,0:T(8,128)S(1)} all-to-all(f32[32,8,128]{2,1,0:T(8,128)S(1)} %get-tuple-element.13), channel_id=1, replica_groups=mesh['rows'=32,'gz'=4] {'rows'}, dimensions={0} | all-to-all | bytes 262144 | tf_op jit(solution)/shard_map/all_to_all | solution.py:519
  86.7 0.0 copy-done.1
  86.7 1.1 %spread.1 = f32[10,16,10]{2,1,0:T(8,128)} custom-call(f32[32,8,128]{2,1,0:T(8,128)S(1)} %all_to_all.10.parts, f32[128,64]{1,0:T(8,128)S(1)} %copy-done.1), custom_call_target="tpu_custom_call" | custom-call | tf_op jit(solution)/shard_map/spread/pallas_call | solution.py:520
Async XLA Ops:
  0.6 0.7 copy-start.2
  9.6 26.4 %collective-permute-start = (f32[26,16,1024]{2,1,0:T(8,128)}, f32[26,16,1024]{2,1,0:T(8,128)S(1)}, u32[]{:S(2)}, u32[]{:S(2)}) collective-permute-start(f32[26,16,1024]{2,1,0:T(8,128)} %get-tuple-element.10), channel_id=1, source_target_pairs={{0,4},{4,8},{8,12},{12,16},{16,20},{20,24},{24,28},{28,32},{32,36}... | collective-permute-start | bytes 5111816 | tf_op jit(solution)/shard_map/ppermute | solution.py:468
  14.1 26.5 %collective-permute-start.1 = (f32[26,16,1024]{2,1,0:T(8,128)}, f32[26,16,1024]{2,1,0:T(8,128)}, u32[]{:S(2)}, u32[]{:S(2)}) collective-permute-start(f32[26,16,1024]{2,1,0:T(8,128)} %get-tuple-element.11), channel_id=1, source_target_pairs={{4,0},{8,4},{12,8},{16,12},{20,16},{24,20},{28,24},{32,28},{36,32}... | collective-permute-start | bytes 5111816 | tf_op jit(solution)/shard_map/ppermute | solution.py:469
  16.0 32.2 %all-to-all-start = ((f32[128,8,128]{2,1,0:T(8,128)}), f32[128,8,128]{2,1,0:T(8,128)S(1)}, u32[]{:S(2)}, u32[]{:S(2)}) async-start(f32[128,8,128]{2,1,0:T(8,128)} %get-tuple-element.9.unused), calls=%async_computation | async-start | bytes 1048576 | tf_op jit(solution)/shard_map/all_to_all | solution.py:470
  26.7 21.6 %copy-start = (f32[160,64]{1,0:T(8,128)S(1)}, f32[160,64]{1,0:T(8,128)}, u32[]{:S(2)}) copy-start(f32[160,64]{1,0:T(8,128)} %constant.4.clone.pick) | copy-start | bytes 122884
  26.7 21.6 %copy-start.3 = (f32[2,10]{1,0:T(2,128)S(1)}, f32[2,10]{1,0:T(2,128)}, u32[]{:S(2)}) copy-start(f32[2,10]{1,0:T(2,128)} %v0.1) | copy-start | bytes 244
  36.0 4.6 %copy-start.4 = (f32[26,16,1024]{2,1,0:T(8,128)}, f32[26,16,1024]{2,1,0:T(8,128)S(1)}, u32[]{:S(2)}) copy-start(f32[26,16,1024]{2,1,0:T(8,128)S(1)} %collective-permute-done.above.edge_above) | copy-start | bytes 5111812
  45.4 41.3 %copy-start.1 = (f32[128,64]{1,0:T(8,128)S(1)}, f32[128,64]{1,0:T(8,128)}, u32[]{:S(2)}) copy-start(f32[128,64]{1,0:T(8,128)} %constant.5.clone.pick) | copy-start | bytes 98308

commit v2 on v1

--- a/solution.py
+++ b/solution.py
@@ -18,6 +18,7 @@
 TILES = NY // 128
 BLOCK = 8
 TALL = WIDE + BLOCK
+CHUNKS = 4
 highest = lax.Precision.HIGHEST
 f32 = jnp.float32
 bf16 = jnp.bfloat16
@@ -112,32 +113,127 @@
     return packed
 
 
-def start_sums(w, e, ph, out, low, high, wt, et, pad, wsem, esem, hsem):
-    half = ROWS // 2
-    chunks, edges = [], []
-    for part, edge in enumerate((high, low)):
-        at = slice(half * part, half * (part + 1))
+def cut_edges(w, e, low, high, raw, lsem, ssem):
+    groups = ((w.at[0:8], 0, 8), (w.at[8:16], 8, 8), (e, 16, 10))
+    loads, stores = [], []
+    for i, (origin, start, count) in enumerate(groups):
+        at = slice(start, start + count)
+        loads.append(pltpu.make_async_copy(origin, raw.at[at], lsem.at[i]))
+        loads[i].start()
+        stores += [
+            pltpu.make_async_copy(raw.at[at, ROWS - HALO : ROWS, :], low.at[at], ssem.at[i, 0]),
+            pltpu.make_async_copy(raw.at[at, 0:HALO, :], high.at[at], ssem.at[i, 1]),
+        ]
+    for i in range(3):
+        loads[i].wait()
+        for copy in stores[2 * i : 2 * i + 2]:
+            copy.start()
+    for copy in stores:
+        copy.wait()
+
+
+def spots(k):
+    return pl.ds(64 * (k % 2) + k // 2, 8, stride=8)
+
+
+def turn_in(value, new, row):
+    stacked = jnp.concatenate([value[:, 128 * t : 128 * t + 128] for t in range(TILES)], axis=0)
+    across = stacked.T
+    for k in range(16):
+        new[row, spots(k), :] = across[8 * k : 8 * k + 8]
+
+
+def turn_out(old, row, new, new_row):
+    across = jnp.concatenate([old[row, spots(k), :] for k in range(16)], axis=0).T
+    for t in range(TILES):
+        new[new_row, :, 128 * t : 128 * t + 128] = across[16 * t : 16 * t + 16]
+
+
+def turn_slab(loads, raw, er, new, warm, modes, ssem):
+    er[:, 8:16, :] = jnp.zeros((ROWS, 8, NY), f32)
+    stores = [
+        pltpu.make_async_copy(er, modes, ssem.at[0]),
+        pltpu.make_async_copy(new, warm, ssem.at[1]),
+    ]
+    for copies in loads:
+        for copy in copies:
+            copy.start()
+    for part, copies in enumerate(loads[:-1]):
+        for copy in copies:
+            copy.wait()
+
+        def step(r, unused):
+            turn_in(raw[HALO * part + r], new, HALO * part + r)
+            return unused
+
+        lax.fori_loop(0, HALO, step, 0, unroll=8)
+    stores[1].start()
+    for copy in loads[-1]:
+        copy.wait()
+    stores[0].start()
+    for copy in stores:
+        copy.wait()
+
+
+def turn_edges(above, below, warm, modes, raw, er, new, lsem, msem, ssem):
+    loads, mode_loads = [], []
+    for side, edge in enumerate((above, below)):
+        at = slice(HALO * side, HALO * side + HALO)
+        loads.append(
+            [
+                pltpu.make_async_copy(edge.at[z], raw.at[at, z, :], lsem.at[side, z])
+                for z in range(ZL)
+            ]
+        )
+        mode_loads += [
+            pltpu.make_async_copy(edge.at[ZL + m], er.at[at, m, :], msem.at[side, m])
+            for m in range(M)
+        ]
+    turn_slab(loads + [mode_loads], raw, er, new, warm, modes, ssem)
+
+
+def start_sums(
+    w, e, ph, unused_low, out, warm, modes, wt, et, tw, pad, phv, wsem, esem, psem, ssem
+):
+    count = ROWS // CHUNKS
+    chunks, stores = [], []
+    for part in range(CHUNKS):
+        at = slice(count * part, count * (part + 1))
         chunks.append(
             [
+                pltpu.make_async_copy(w.at[z, at, :], wt.at[at, z, :], wsem.at[part, z])
+                for z in range(ZL)
+            ]
+            + [
                 pltpu.make_async_copy(e.at[m, at, :], et.at[at, m, :], esem.at[part, m])
                 for m in range(M)
             ]
-            + [
-                pltpu.make_async_copy(w.at[z, at, :], wt.at[at, z, :], wsem.at[part, z])
-                for z in range(ZL)
+        )
+        stores.append(
+            [
+                pltpu.make_async_copy(et.at[at], modes.at[at], ssem.at[part, 0]),
+                pltpu.make_async_copy(tw.at[at], warm.at[at], ssem.at[part, 1]),
             ]
         )
-        edges += [
-            pltpu.make_async_copy(wt.at[at, z, :], edge.at[z], hsem.at[part, z]) for z in range(ZL)
-        ] + [
-            pltpu.make_async_copy(et.at[at, m, :], edge.at[ZL + m], hsem.at[part, ZL + m])
-            for m in range(M)
-        ]
+    et[:, 8:16, :] = jnp.zeros((ROWS, 8, NY), f32)
     for copies in chunks:
         for copy in copies:
             copy.start()
+    phase_copy = pltpu.make_async_copy(ph, phv, psem)
+    phase_copy.start()
+    acc = jnp.zeros((128, 32), f32)
+    for part, copies in enumerate(chunks):
+        for copy in copies:
+            copy.wait()
+        stores[part][0].start()
+        start = count * part
+        for r in range(start, start + count):
+            turn_in(wt[r], tw, r)
+        acc = sums_of_rows(wt, start, et, start, count, count, acc)
+        stores[part][1].start()
+    phase_copy.wait()
     pad[...] = jnp.zeros((128, 128), f32)
-    pad[0:ZL, 0:M] = ph[...]
+    pad[0:ZL, 0:M] = phv[...]
     turned = pad[...].T
     row = lax.broadcasted_iota(jnp.int32, (64, 128), 0)
     phases = jnp.zeros((64, 128), f32)
@@ -146,66 +242,10 @@
             row == place, jnp.broadcast_to(turned[m : m + 1, :], (64, 128)), 0.0
         )
     phases = phases * jnp.where(lax.axis_index("rows") == 0, 1.0, 0.0)
-    acc = jnp.zeros((128, 32), f32)
-    for part, copies in enumerate(chunks):
+    out[...] = packed_sums(acc, pad, 2.0 / float(NX * NY), phases)
+    for copies in stores:
         for copy in copies:
             copy.wait()
-        for copy in edges[(ZL + M) * part : (ZL + M) * (part + 1)]:
-            copy.start()
-        acc = sums_of_rows(wt, half * part, et, half * part, half, 16, acc)
-    packed = packed_sums(acc, pad, 2.0 / float(NX * NY), phases)
-    out[...] = jnp.broadcast_to(packed[None], out.shape)
-    for copy in edges:
-        copy.wait()
-
-
-def spots(k):
-    return pl.ds(64 * (k % 2) + k // 2, 8, stride=8)
-
-
-def turn_in(value, new, row):
-    stacked = jnp.concatenate([value[:, 128 * t : 128 * t + 128] for t in range(TILES)], axis=0)
-    across = stacked.T
-    for k in range(16):
-        new[row, spots(k), :] = across[8 * k : 8 * k + 8]
-
-
-def turn_out(old, row, new, new_row):
-    across = jnp.concatenate([old[row, spots(k), :] for k in range(16)], axis=0).T
-    for t in range(TILES):
-        new[new_row, :, 128 * t : 128 * t + 128] = across[16 * t : 16 * t + 16]
-
-
-def turn_warming(w, above, below, unused, out, raw, new, lsem, ssem):
-    sides = (
-        (w, HALO, ROWS),
-        (above, 0, HALO),
-        (below, HALO + ROWS, HALO),
-    )
-    loads, stores = [], []
-    for side, (origin, start, count) in enumerate(sides):
-        at = slice(start, start + count)
-        loads.append(
-            [
-                pltpu.make_async_copy(origin.at[z], raw.at[at, z, :], lsem.at[side, z])
-                for z in range(ZL)
-            ]
-        )
-        stores.append(pltpu.make_async_copy(new.at[at], out.at[at], ssem.at[side]))
-        for copy in loads[side]:
-            copy.start()
-    for side, (origin, start, count) in enumerate(sides):
-        for copy in loads[side]:
-            copy.wait()
-
-        def step(r, unused):
-            turn_in(raw[start + r], new, start + r)
-            return unused
-
-        lax.fori_loop(0, count, step, 0, unroll=8)
-        stores[side].start()
-    for copy in stores:
-        copy.wait()
 
 
 def row_of(ref, *index):
@@ -217,7 +257,7 @@
     totals = []
     for q in range(GZ):
         total = parts[q]
-        for r in range(1, 32):
+        for r in range(1, parts.shape[0] // GZ):
             total = total + parts[GZ * r + q]
         totals.append(total)
     rows = []
@@ -365,30 +405,33 @@
 
 
 def heat_and_sums(
-    parts, warm, e, edge_above, edge_below, pick, v0,
+    parts, warm, modes, edge_warm, edge_modes, pick, v0,
     field, out, incoming,
     f0, f1, source, et, plain, cs, ts, square, wsem, esem, osem,
 ):
-    warm_copy = pltpu.make_async_copy(warm, f0.at[0:WIDE], wsem)
-    mode_copies = []
-    for m in range(M):
-        for side, (origin, at) in enumerate(
-            (
-                (e.at[m], slice(HALO, HALO + ROWS)),
-                (edge_above.at[ZL + m], slice(0, HALO)),
-                (edge_below.at[ZL + m], slice(HALO + ROWS, WIDE)),
-            )
-        ):
-            mode_copies.append(pltpu.make_async_copy(origin, et.at[at, m, :], esem.at[side, m]))
-    et[:, 8:16, :] = jnp.zeros((WIDE, 8, NY), f32)
+    own = slice(HALO, HALO + ROWS)
+    above, below = slice(0, HALO), slice(HALO + ROWS, WIDE)
+    mode_copies, copies = [
+        [
+            pltpu.make_async_copy(inner, wide.at[own], sem.at[0]),
+            pltpu.make_async_copy(outer.at[0:HALO], wide.at[above], sem.at[1]),
+            pltpu.make_async_copy(outer.at[HALO : 2 * HALO], wide.at[below], sem.at[2]),
+        ]
+        for inner, outer, wide, sem in (
+            (modes, edge_modes, et, esem),
+            (warm, edge_warm, f0, wsem),
+        )
+    ]
     for copy in mode_copies:
         copy.start()
-    warm_copy.start()
     real, imag = amplitudes(parts, pick, v0, cs, ts, square, incoming)
     for copy in mode_copies:
         copy.wait()
+    for copy in copies:
+        copy.start()
     heat_load(real, imag, et, source)
-    warm_copy.wait()
+    for copy in copies:
+        copy.wait()
     place = lax.axis_index("rows")
     first = place == 0
     last = place == lax.axis_size("rows") - 1
@@ -447,41 +490,58 @@
     edge = pltpu.HBM((ZL + M, HALO, NY), f32)
     slab_vmem = pltpu.VMEM((ROWS, 16, NY), f32)
     warming, shapes = on_hbm(segment_warming), on_hbm(eigenfunction_crosssections)
-    packed, low, high = pl.pallas_call(
+    low, high = pl.pallas_call(
+        cut_edges,
+        name="cut_edges",
+        out_shape=(edge, edge),
+        in_specs=[hbm, hbm],
+        out_specs=(hbm, hbm),
+        scratch_shapes=[pltpu.VMEM((ZL + M, ROWS, NY), f32), dma((3,)), dma((3, 2))],
+        compiler_params=pltpu.CompilerParams(vmem_limit_bytes=16 << 20),
+    )(warming, shapes)
+    forward = [(i, i + 1) for i in range(devices - 1)]
+    backward = [(target, origin) for origin, target in forward]
+    slab = (pltpu.HBM((ROWS, 128, 128), f32), pltpu.HBM((ROWS, 16, NY), f32))
+    packed, warm, modes = pl.pallas_call(
         start_sums,
         name="start_sums",
-        out_shape=(jax.ShapeDtypeStruct((devices * GZ, 8, 128), f32), edge, edge),
-        in_specs=[hbm, hbm, vmem],
+        out_shape=(jax.ShapeDtypeStruct((8, 128), f32),) + slab,
+        in_specs=[hbm, hbm, hbm, hbm],
         out_specs=(vmem, hbm, hbm),
         scratch_shapes=[
             slab_vmem,
             slab_vmem,
+            pltpu.VMEM((ROWS, 128, 128), f32),
             pltpu.VMEM((128, 128), f32),
-            dma((2, ZL)),
-            dma((2, M)),
-            dma((2, ZL + M)),
+            pltpu.VMEM((ZL, M), f32),
+            dma((CHUNKS, ZL)),
+            dma((CHUNKS, M)),
+            dma,
+            dma((CHUNKS, 2)),
         ],
-        compiler_params=pltpu.CompilerParams(vmem_limit_bytes=16 << 20),
-    )(warming, shapes, segment_phasors)
-    forward = [(i, i + 1) for i in range(devices - 1)]
-    backward = [(target, origin) for origin, target in forward]
+        compiler_params=pltpu.CompilerParams(vmem_limit_bytes=24 << 20),
+    )(warming, shapes, on_hbm(segment_phasors), on_hbm(low))
+    mate = lax.ppermute(packed, "rows", [(i, i ^ 1) for i in range(devices)])
     above = lax.ppermute(low, "rows", forward)
     below = lax.ppermute(high, "rows", backward)
-    parts = lax.all_to_all(packed, ("rows", "gz"), 0, 0, tiled=True)
-    warm = pl.pallas_call(
-        turn_warming,
-        name="turn_warming",
-        out_shape=pltpu.HBM((WIDE, 128, 128), f32),
-        in_specs=[hbm, hbm, hbm, pl.BlockSpec(memory_space=pl.ANY)],
-        out_specs=hbm,
-        scratch_shapes=[
-            pltpu.VMEM((WIDE, ZL, NY), f32),
-            pltpu.VMEM((WIDE, 128, 128), f32),
-            dma((3, ZL)),
-            dma((3,)),
-        ],
+    both = jnp.broadcast_to((packed + mate)[None], (devices * GZ // 2, 8, 128))
+    groups = [
+        [GZ * (2 * chip + core) + q for chip in range(devices // 2) for q in range(GZ)]
+        for core in range(2)
+    ]
+    parts = lax.all_to_all(
+        both, ("rows", "gz"), 0, 0, axis_index_groups=groups, tiled=True
+    )
+    turn_scratch = [slab_vmem, slab_vmem, pltpu.VMEM((ROWS, 128, 128), f32)]
+    edge_warm, edge_modes = pl.pallas_call(
+        turn_edges,
+        name="turn_edges",
+        out_shape=slab,
+        in_specs=[hbm, hbm],
+        out_specs=(hbm, hbm),
+        scratch_shapes=turn_scratch + [dma((2, ZL)), dma((2, M)), dma((2,))],
         compiler_params=pltpu.CompilerParams(vmem_limit_bytes=16 << 20),
-    )(warming, on_hbm(above), on_hbm(below), packed)
+    )(on_hbm(above), on_hbm(below))
     wide_vmem = pltpu.VMEM((TALL, 128, 128), f32)
     field, packed, incoming = pl.pallas_call(
         heat_and_sums,
@@ -502,17 +562,17 @@
             pltpu.VMEM((160, 128), f32),
             pltpu.VMEM((6, 2, 160, 128), f32),
             pltpu.VMEM((128, 128), f32),
-            dma,
-            dma((3, M)),
+            dma((3,)),
+            dma((3,)),
             dma((ROWS // 8, ZL)),
         ],
         compiler_params=pltpu.CompilerParams(vmem_limit_bytes=40 << 20),
     )(
         parts,
         on_hbm(warm),
-        shapes,
-        on_hbm(above),
-        on_hbm(below),
+        on_hbm(modes),
+        on_hbm(edge_warm),
+        on_hbm(edge_modes),
         jnp.asarray(selection(16, 160)),
         injected_coefficients,
     )

time: 88.1 us -> 80.5 us (0.914)
  waiting for transfers between devices: 16.7 us -> 5.13 us
  Pallas kernels: 37.4 us -> 40.5 us
  blocking collectives: 15.2 us -> 12.2 us
  starting transfers between devices: 17.1 us -> 19.8 us
  local copies, waits for them, and re-layouts: 0.71 us -> 1.89 us
    ppermute x1, waiting for transfers between devices: 9.27 us -> 0.01 us  [shards(): above = lax.ppermute(low, 'rows', forward)]
    ppermute x1, waiting for transfers between devices: 4.58 us -> 0.01 us  [shards(): below = lax.ppermute(high, 'rows', backward)]
    all_to_all x1, blocking collectives: 15.2 us -> 12.2 us  [shards(): parts = lax.all_to_all(packed, 'rows', 0, 0, tiled=True)]
    pallas_call x1 -> x2, Pallas kernels: 4.85 us -> 7.72 us  [the longest x1 4.59 us: shards(): pl.pallas_call(turn_edges, name='turn_edges', out_shape=slab, in_specs=[h...]
    all_to_all x1, starting transfers between devices: 10.6 us -> 12.7 us  [shards(): lax.all_to_all(both, ('rows', 'gz'), 0, 0, axis_index_groups=groups, tile...]
    all_to_all x1, waiting for transfers between devices: 2.8 us -> 4.3 us  [shards(): lax.all_to_all(both, ('rows', 'gz'), 0, 0, axis_index_groups=groups, tile...]
    ppermute x1, starting transfers between devices: 1.92 us -> 3.29 us  [shards(): below = lax.ppermute(high, 'rows', backward)]
    ppermute x1, starting transfers between devices: 4.5 us -> 3.13 us  [shards(): above = lax.ppermute(low, 'rows', forward)]
  transfers between devices with their start and end apart: 3 -> 4, of which waited for: 3 -> 2; matrix products, arithmetic and copies ran while one was open for 0% -> 1% of each run, Pallas kernels for 6% -> 15%
where the time goes in v2:
time: 80.5 us; the launch traced here: 80.2 us
  Pallas kernels  40.5 us (50%)
  starting transfers between devices  19.8 us (25%)
  blocking collectives  12.2 us (15%)
  waiting for transfers between devices  5.13 us (6%)
  local copies, waits for them, and re-layouts  1.89 us (2%)
    pallas_call x1, Pallas kernels, shards(): pl.pallas_call(heat_and_sums, name='heat_and_sums', out_shape=(jax.ShapeD...  24 us
    all_to_all x1, starting transfers between devices, shards(): lax.all_to_all(both, ('rows', 'gz'), 0, 0, axis_index_groups=groups, tile...  12.7 us
    all_to_all x1, blocking collectives, shards(): parts = lax.all_to_all(packed, 'rows', 0, 0, tiled=True)  12.2 us
    pallas_call x1, Pallas kernels, shards(): pl.pallas_call(start_sums, name='start_sums', out_shape=(jax.ShapeDtypeSt...  7.63 us
    pallas_call x1, Pallas kernels, shards(): pl.pallas_call(turn_edges, name='turn_edges', out_shape=slab, in_specs=[h...  4.59 us
    all_to_all x1, waiting for transfers between devices, shards(): lax.all_to_all(both, ('rows', 'gz'), 0, 0, axis_index_groups=groups, tile...  4.3 us
    ppermute x1, starting transfers between devices, shards(): below = lax.ppermute(high, 'rows', backward)  3.29 us
    ppermute x1, starting transfers between devices, shards(): above = lax.ppermute(low, 'rows', forward)  3.13 us
  transfers between devices with their start and end apart: 4, of which 2 were waited for; matrix products, arithmetic and copies ran while one was open for 1% of the time, Pallas kernels for 15%

profile of v2, /device:TPU:1, one launch (start us, length us, event | category | flops | bytes accessed | tf_op | source)
XLA Modules:
  0.0 80.2 jit_solution(7709475526005201242)
XLA Ops:
  0.6 3.1 %cut_edges.1 = (f32[26,16,1024]{2,1,0:T(8,128)}, f32[26,16,1024]{2,1,0:T(8,128)}) custom-call(f32[16,32,1024]{2,1,0:T(8,128)} %w.3, f32[10,32,1024]{2,1,0:T(8,128)} %e.3), custom_call_target="tpu_custom_call" | custom-call | tf_op jit(solution)/shard_map/cut_edges/pallas_call | solution.py:493
  3.8 3.3 %collective-permute-start.2 = (f32[26,16,1024]{2,1,0:T(8,128)}, f32[26,16,1024]{2,1,0:T(8,128)S(1)}, u32[]{:S(2)}, u32[]{:S(2)}) collective-permute-start(f32[26,16,1024]{2,1,0:T(8,128)} %get-tuple-element.17), channel_id=1, source_target_pairs={{4,0},{8,4},{12,8},{16,12},{20,16},{24,20},{28,24},{32,28},{36,32}... | collective-permute-start | bytes 5111816 | tf_op jit(solution)/shard_map/ppermute | solution.py:526
  7.1 3.1 %collective-permute-start.1 = (f32[26,16,1024]{2,1,0:T(8,128)}, f32[26,16,1024]{2,1,0:T(8,128)}, u32[]{:S(2)}, u32[]{:S(2)}) collective-permute-start(f32[26,16,1024]{2,1,0:T(8,128)} %get-tuple-element.13.unused_low), channel_id=1, source_target_pairs={{0,4},{4,8},{8,12},{12,16},{16,20},{20,24},{24,28},{28,32},{32,36}... | collective-permute-start | bytes 5111816 | tf_op jit(solution)/shard_map/ppermute | solution.py:525
  10.2 7.6 %start_sums.1 = (f32[8,128]{1,0:T(8,128)S(1)}, f32[32,128,128]{2,1,0:T(8,128)}, f32[32,16,1024]{2,1,0:T(8,128)}) custom-call(f32[16,32,1024]{2,1,0:T(8,128)} %w.3, f32[10,32,1024]{2,1,0:T(8,128)} %e.3, f32[16,10]{1,0:T(8,128)} %ph.1, f32[26,16,1024]{2,1,0:T(8,128)} %get-tuple-element.13.unused_low), custom_call_target="tpu_custom_call" | custom-call | tf_op jit(solution)/shard_map/start_sums/pallas_call | solution.py:505
  17.8 0.6 collective-permute-start
  18.5 0.8 %collective-permute-done = f32[8,128]{1,0:T(8,128)S(1)} collective-permute-done((f32[8,128]{1,0:T(8,128)S(1)}, f32[8,128]{1,0:T(8,128)S(1)}, u32[]{:S(2)}, u32[]{:S(2)}) %collective-permute-start) | collective-permute-done | bytes 4128 | tf_op jit(solution)/shard_map/ppermute | solution.py:524
  19.3 0.0 copy-start
  19.3 0.0 copy-start.2
  19.3 0.7 broadcast_in_dim.2
  20.0 12.7 %all-to-all-start = ((f32[64,8,128]{2,1,0:T(8,128)}), f32[64,8,128]{2,1,0:T(8,128)S(1)}, u32[]{:S(2)}, u32[]{:S(2)}) async-start(f32[64,8,128]{2,1,0:T(8,128)} %broadcast_in_dim.2), calls=%async_computation | async-start | bytes 524288 | tf_op jit(solution)/shard_map/all_to_all | solution.py:532
  32.8 0.0 collective-permute-done.2.below
  32.8 0.0 copy-start.3
  32.8 0.0 collective-permute-done.1.above
  32.8 1.2 %copy-done.3 = f32[26,16,1024]{2,1,0:T(8,128)} copy-done((f32[26,16,1024]{2,1,0:T(8,128)}, f32[26,16,1024]{2,1,0:T(8,128)S(1)}, u32[]{:S(2)}) %copy-start.3) | copy-done | bytes 1703960
  34.0 4.6 %turn_edges.1 = (f32[32,128,128]{2,1,0:T(8,128)}, f32[32,16,1024]{2,1,0:T(8,128)}) custom-call(f32[26,16,1024]{2,1,0:T(8,128)} %collective-permute-done.1.above, f32[26,16,1024]{2,1,0:T(8,128)} %copy-done.3), custom_call_target="tpu_custom_call" | custom-call | tf_op jit(solution)/shard_map/turn_edges/pallas_call | solution.py:536
  38.6 4.3 %all-to-all-done.parts = f32[64,8,128]{2,1,0:T(8,128)S(1)} async-done(((f32[64,8,128]{2,1,0:T(8,128)}), f32[64,8,128]{2,1,0:T(8,128)S(1)}, u32[]{:S(2)}, u32[]{:S(2)}) %all-to-all-start) | async-done | bytes 262176 | tf_op jit(solution)/shard_map/all_to_all | solution.py:532
  42.9 0.0 copy-done
  42.9 0.0 copy-done.2
  42.9 0.0 copy-start.1
  42.9 24.0 %heat_and_sums.1 = (f32[16,32,1024]{2,1,0:T(8,128)}, f32[32,8,128]{2,1,0:T(8,128)S(1)}, f32[10,2,16]{2,1,0:T(2,128)}) custom-call(f32[64,8,128]{2,1,0:T(8,128)S(1)} %all-to-all-done.parts, f32[32,128,128]{2,1,0:T(8,128)} %get-tuple-element.15.warm, f32[32,16,1024]{2,1,0:T(8,128)} %get-tuple-element.16.modes, f32[32,128,128]{2,1,0:T(8,128)} %get-tuple-element.18.edge_warm, ...), custom_call_target="tpu_custom_call" | custom-call | tf_op jit(solution)/shard_map/heat_and_sums/pallas_call | solution.py:546
  66.9 12.2 %all_to_all.10.parts = f32[32,8,128]{2,1,0:T(8,128)S(1)} all-to-all(f32[32,8,128]{2,1,0:T(8,128)S(1)} %get-tuple-element.21), channel_id=1, replica_groups=mesh['rows'=32,'gz'=4] {'rows'}, dimensions={0} | all-to-all | bytes 262144 | tf_op jit(solution)/shard_map/all_to_all | solution.py:579
  79.1 0.0 copy-done.1
  79.1 1.1 %spread.1 = f32[10,16,10]{2,1,0:T(8,128)} custom-call(f32[32,8,128]{2,1,0:T(8,128)S(1)} %all_to_all.10.parts, f32[128,64]{1,0:T(8,128)S(1)} %copy-done.1), custom_call_target="tpu_custom_call" | custom-call | tf_op jit(solution)/shard_map/spread/pallas_call | solution.py:580
  (1 shorter events, 0.0 us)
Async XLA Ops:
  3.8 29.0 %collective-permute-start.2 = (f32[26,16,1024]{2,1,0:T(8,128)}, f32[26,16,1024]{2,1,0:T(8,128)S(1)}, u32[]{:S(2)}, u32[]{:S(2)}) collective-permute-start(f32[26,16,1024]{2,1,0:T(8,128)} %get-tuple-element.17), channel_id=1, source_target_pairs={{4,0},{8,4},{12,8},{16,12},{20,16},{24,20},{28,24},{32,28},{36,32}... | collective-permute-start | bytes 5111816 | tf_op jit(solution)/shard_map/ppermute | solution.py:526
  7.1 25.7 %collective-permute-start.1 = (f32[26,16,1024]{2,1,0:T(8,128)}, f32[26,16,1024]{2,1,0:T(8,128)}, u32[]{:S(2)}, u32[]{:S(2)}) collective-permute-start(f32[26,16,1024]{2,1,0:T(8,128)} %get-tuple-element.13.unused_low), channel_id=1, source_target_pairs={{0,4},{4,8},{8,12},{12,16},{16,20},{20,24},{24,28},{28,32},{32,36}... | collective-permute-start | bytes 5111816 | tf_op jit(solution)/shard_map/ppermute | solution.py:525
  17.8 1.4 %collective-permute-start = (f32[8,128]{1,0:T(8,128)S(1)}, f32[8,128]{1,0:T(8,128)S(1)}, u32[]{:S(2)}, u32[]{:S(2)}) collective-permute-start(f32[8,128]{1,0:T(8,128)S(1)} %get-tuple-element.14), channel_id=1, source_target_pairs={{0,4},{4,0},{8,12},{12,8},{16,20},{20,16},{24,28},{28,24},{32,36},... | collective-permute-start | bytes 12296 | tf_op jit(solution)/shard_map/ppermute | solution.py:524
  19.3 23.6 %copy-start = (f32[160,64]{1,0:T(8,128)S(1)}, f32[160,64]{1,0:T(8,128)}, u32[]{:S(2)}) copy-start(f32[160,64]{1,0:T(8,128)} %constant.4.clone.pick) | copy-start | bytes 122884
  19.3 23.6 %copy-start.2 = (f32[2,10]{1,0:T(2,128)S(1)}, f32[2,10]{1,0:T(2,128)}, u32[]{:S(2)}) copy-start(f32[2,10]{1,0:T(2,128)} %v0.1) | copy-start | bytes 244
  20.0 22.8 %all-to-all-start = ((f32[64,8,128]{2,1,0:T(8,128)}), f32[64,8,128]{2,1,0:T(8,128)S(1)}, u32[]{:S(2)}, u32[]{:S(2)}) async-start(f32[64,8,128]{2,1,0:T(8,128)} %broadcast_in_dim.2), calls=%async_computation | async-start | bytes 524288 | tf_op jit(solution)/shard_map/all_to_all | solution.py:532
  32.8 1.2 %copy-start.3 = (f32[26,16,1024]{2,1,0:T(8,128)}, f32[26,16,1024]{2,1,0:T(8,128)S(1)}, u32[]{:S(2)}) copy-start(f32[26,16,1024]{2,1,0:T(8,128)S(1)} %collective-permute-done.2.below) | copy-start | bytes 5111812
  42.9 36.2 %copy-start.1 = (f32[128,64]{1,0:T(8,128)S(1)}, f32[128,64]{1,0:T(8,128)}, u32[]{:S(2)}) copy-start(f32[128,64]{1,0:T(8,128)} %constant.5.clone.pick) | copy-start | bytes 98308

commit v3 on v2

--- a/solution.py
+++ b/solution.py
@@ -216,21 +216,11 @@
             ]
         )
     et[:, 8:16, :] = jnp.zeros((ROWS, 8, NY), f32)
+    phase_copy = pltpu.make_async_copy(ph, phv, psem)
+    phase_copy.start()
     for copies in chunks:
         for copy in copies:
             copy.start()
-    phase_copy = pltpu.make_async_copy(ph, phv, psem)
-    phase_copy.start()
-    acc = jnp.zeros((128, 32), f32)
-    for part, copies in enumerate(chunks):
-        for copy in copies:
-            copy.wait()
-        stores[part][0].start()
-        start = count * part
-        for r in range(start, start + count):
-            turn_in(wt[r], tw, r)
-        acc = sums_of_rows(wt, start, et, start, count, count, acc)
-        stores[part][1].start()
     phase_copy.wait()
     pad[...] = jnp.zeros((128, 128), f32)
     pad[0:ZL, 0:M] = phv[...]
@@ -242,6 +232,16 @@
             row == place, jnp.broadcast_to(turned[m : m + 1, :], (64, 128)), 0.0
         )
     phases = phases * jnp.where(lax.axis_index("rows") == 0, 1.0, 0.0)
+    acc = jnp.zeros((128, 32), f32)
+    for part, copies in enumerate(chunks):
+        for copy in copies:
+            copy.wait()
+        stores[part][0].start()
+        start = count * part
+        for r in range(start, start + count):
+            turn_in(wt[r], tw, r)
+        acc = sums_of_rows(wt, start, et, start, count, count, acc)
+        stores[part][1].start()
     out[...] = packed_sums(acc, pad, 2.0 / float(NX * NY), phases)
     for copies in stores:
         for copy in copies:
@@ -382,6 +382,7 @@
                 return old[row, 8 * v : 8 * v + 8, :]
 
             rows = [{v: register(r - 1 + i, v) for v in some} for i in range(BLOCK + 2)]
+            middle = {}
             for i in range(BLOCK):
                 center = dict(rows[i + 1])
                 if half == 0:
@@ -396,7 +397,10 @@
                     center[7] = register(r + i, 7)
                 for v in some:
                     sides = center[v - 1] + center[v + 1]
-                    total = (rows[i][v] + center[v]) + (rows[i + 2][v] + sides)
+                    if i % 2 == 0:
+                        middle[v] = center[v] + rows[i + 2][v]
+                    outer = rows[i][v] if i % 2 == 0 else rows[i + 2][v]
+                    total = (outer + middle[v]) + sides
                     cut = slice(8 * v, 8 * v + 8)
                     new[r + i, cut, :] = 0.2 * total + source[r + i, cut, :]
         return unused
@@ -459,7 +463,7 @@
             copy = pltpu.make_async_copy(plain.at[at, z, :], field.at[z, at, :], osem.at[part, z])
             copy.start()
             outs.append(copy)
-    acc = sums_of_rows(plain, 0, et, HALO, ROWS, 16, jnp.zeros((128, 32), f32))
+    acc = sums_of_rows(plain, 0, et, HALO, ROWS, 32, jnp.zeros((128, 32), f32))
     packed = packed_sums(acc, square, 1.0 / float(NX * NY), None)
     out[...] = jnp.broadcast_to(packed[None], out.shape)
     for copy in outs:

time: 80.5 us -> 79.6 us (0.989)
  Pallas kernels: 40.5 us -> 39.5 us
    pallas_call x1, Pallas kernels: 24 us -> 22.8 us  [shards(): pl.pallas_call(heat_and_sums, name='heat_and_sums', out_shape=(jax.ShapeD...]
  transfers between devices with their start and end apart: 4 -> 4, of which waited for: 2 -> 2; matrix products, arithmetic and copies ran while one was open for 1% -> 1% of each run, Pallas kernels for 15% -> 16%
where the time goes in v3:
time: 79.6 us; the launch traced here: 79.2 us
  Pallas kernels  39.5 us (50%)
  starting transfers between devices  19.8 us (25%)
  blocking collectives  12.2 us (15%)
  waiting for transfers between devices  5.13 us (6%)
  local copies, waits for them, and re-layouts  1.89 us (2%)
    pallas_call x1, Pallas kernels, shards(): pl.pallas_call(heat_and_sums, name='heat_and_sums', out_shape=(jax.ShapeD...  22.8 us
    all_to_all x1, starting transfers between devices, shards(): lax.all_to_all(both, ('rows', 'gz'), 0, 0, axis_index_groups=groups, tile...  12.7 us
    all_to_all x1, blocking collectives, shards(): parts = lax.all_to_all(packed, 'rows', 0, 0, tiled=True)  12.2 us
    pallas_call x1, Pallas kernels, shards(): pl.pallas_call(start_sums, name='start_sums', out_shape=(jax.ShapeDtypeSt...  7.91 us
    pallas_call x1, Pallas kernels, shards(): pl.pallas_call(turn_edges, name='turn_edges', out_shape=slab, in_specs=[h...  4.59 us
    all_to_all x1, waiting for transfers between devices, shards(): lax.all_to_all(both, ('rows', 'gz'), 0, 0, axis_index_groups=groups, tile...  4.3 us
    ppermute x1, starting transfers between devices, shards(): below = lax.ppermute(high, 'rows', backward)  3.29 us
    ppermute x1, starting transfers between devices, shards(): above = lax.ppermute(low, 'rows', forward)  3.13 us
  transfers between devices with their start and end apart: 4, of which 2 were waited for; matrix products, arithmetic and copies ran while one was open for 1% of the time, Pallas kernels for 16%

profile of v3, /device:TPU:1, one launch (start us, length us, event | category | flops | bytes accessed | tf_op | source)
XLA Modules:
  0.0 79.2 jit_solution(5806086022990307577)
XLA Ops:
  0.6 3.1 %cut_edges.1 = (f32[26,16,1024]{2,1,0:T(8,128)}, f32[26,16,1024]{2,1,0:T(8,128)}) custom-call(f32[16,32,1024]{2,1,0:T(8,128)} %w.3, f32[10,32,1024]{2,1,0:T(8,128)} %e.3), custom_call_target="tpu_custom_call" | custom-call | tf_op jit(solution)/shard_map/cut_edges/pallas_call | solution.py:497
  3.8 3.3 %collective-permute-start.2 = (f32[26,16,1024]{2,1,0:T(8,128)}, f32[26,16,1024]{2,1,0:T(8,128)S(1)}, u32[]{:S(2)}, u32[]{:S(2)}) collective-permute-start(f32[26,16,1024]{2,1,0:T(8,128)} %get-tuple-element.17), channel_id=1, source_target_pairs={{4,0},{8,4},{12,8},{16,12},{20,16},{24,20},{28,24},{32,28},{36,32}... | collective-permute-start | bytes 5111816 | tf_op jit(solution)/shard_map/ppermute | solution.py:530
  7.1 3.1 %collective-permute-start.1 = (f32[26,16,1024]{2,1,0:T(8,128)}, f32[26,16,1024]{2,1,0:T(8,128)}, u32[]{:S(2)}, u32[]{:S(2)}) collective-permute-start(f32[26,16,1024]{2,1,0:T(8,128)} %get-tuple-element.13.unused_low), channel_id=1, source_target_pairs={{0,4},{4,8},{8,12},{12,16},{16,20},{20,24},{24,28},{28,32},{32,36}... | collective-permute-start | bytes 5111816 | tf_op jit(solution)/shard_map/ppermute | solution.py:529
  10.2 7.9 %start_sums.1 = (f32[8,128]{1,0:T(8,128)S(1)}, f32[32,128,128]{2,1,0:T(8,128)}, f32[32,16,1024]{2,1,0:T(8,128)}) custom-call(f32[16,32,1024]{2,1,0:T(8,128)} %w.3, f32[10,32,1024]{2,1,0:T(8,128)} %e.3, f32[16,10]{1,0:T(8,128)} %ph.1, f32[26,16,1024]{2,1,0:T(8,128)} %get-tuple-element.13.unused_low), custom_call_target="tpu_custom_call" | custom-call | tf_op jit(solution)/shard_map/start_sums/pallas_call | solution.py:509
  18.1 0.6 collective-permute-start
  18.7 0.8 %collective-permute-done = f32[8,128]{1,0:T(8,128)S(1)} collective-permute-done((f32[8,128]{1,0:T(8,128)S(1)}, f32[8,128]{1,0:T(8,128)S(1)}, u32[]{:S(2)}, u32[]{:S(2)}) %collective-permute-start) | collective-permute-done | bytes 4128 | tf_op jit(solution)/shard_map/ppermute | solution.py:528
  19.6 0.0 copy-start
  19.6 0.0 copy-start.2
  19.6 0.7 broadcast_in_dim.2
  20.3 12.7 %all-to-all-start = ((f32[64,8,128]{2,1,0:T(8,128)}), f32[64,8,128]{2,1,0:T(8,128)S(1)}, u32[]{:S(2)}, u32[]{:S(2)}) async-start(f32[64,8,128]{2,1,0:T(8,128)} %broadcast_in_dim.2), calls=%async_computation | async-start | bytes 524288 | tf_op jit(solution)/shard_map/all_to_all | solution.py:536
  33.0 0.0 collective-permute-done.2.below
  33.0 0.0 copy-start.3
  33.1 0.0 collective-permute-done.1.above
  33.1 1.2 %copy-done.3 = f32[26,16,1024]{2,1,0:T(8,128)} copy-done((f32[26,16,1024]{2,1,0:T(8,128)}, f32[26,16,1024]{2,1,0:T(8,128)S(1)}, u32[]{:S(2)}) %copy-start.3) | copy-done | bytes 1703960
  34.2 4.6 %turn_edges.1 = (f32[32,128,128]{2,1,0:T(8,128)}, f32[32,16,1024]{2,1,0:T(8,128)}) custom-call(f32[26,16,1024]{2,1,0:T(8,128)} %collective-permute-done.1.above, f32[26,16,1024]{2,1,0:T(8,128)} %copy-done.3), custom_call_target="tpu_custom_call" | custom-call | tf_op jit(solution)/shard_map/turn_edges/pallas_call | solution.py:540
  38.8 4.3 %all-to-all-done.parts = f32[64,8,128]{2,1,0:T(8,128)S(1)} async-done(((f32[64,8,128]{2,1,0:T(8,128)}), f32[64,8,128]{2,1,0:T(8,128)S(1)}, u32[]{:S(2)}, u32[]{:S(2)}) %all-to-all-start) | async-done | bytes 262176 | tf_op jit(solution)/shard_map/all_to_all | solution.py:536
  43.1 0.0 copy-done
  43.1 0.0 copy-done.2
  43.1 0.0 copy-start.1
  43.1 22.8 %heat_and_sums.1 = (f32[16,32,1024]{2,1,0:T(8,128)}, f32[32,8,128]{2,1,0:T(8,128)S(1)}, f32[10,2,16]{2,1,0:T(2,128)}) custom-call(f32[64,8,128]{2,1,0:T(8,128)S(1)} %all-to-all-done.parts, f32[32,128,128]{2,1,0:T(8,128)} %get-tuple-element.15.warm, f32[32,16,1024]{2,1,0:T(8,128)} %get-tuple-element.16.modes, f32[32,128,128]{2,1,0:T(8,128)} %get-tuple-element.18.edge_warm, ...), custom_call_target="tpu_custom_call" | custom-call | tf_op jit(solution)/shard_map/heat_and_sums/pallas_call | solution.py:550
  66.0 12.2 %all_to_all.10.parts = f32[32,8,128]{2,1,0:T(8,128)S(1)} all-to-all(f32[32,8,128]{2,1,0:T(8,128)S(1)} %get-tuple-element.21), channel_id=1, replica_groups=mesh['rows'=32,'gz'=4] {'rows'}, dimensions={0} | all-to-all | bytes 262144 | tf_op jit(solution)/shard_map/all_to_all | solution.py:583
  78.2 0.0 copy-done.1
  78.2 1.1 %spread.1 = f32[10,16,10]{2,1,0:T(8,128)} custom-call(f32[32,8,128]{2,1,0:T(8,128)S(1)} %all_to_all.10.parts, f32[128,64]{1,0:T(8,128)S(1)} %copy-done.1), custom_call_target="tpu_custom_call" | custom-call | tf_op jit(solution)/shard_map/spread/pallas_call | solution.py:584
  (1 shorter events, 0.0 us)
Async XLA Ops:
  3.8 29.3 %collective-permute-start.2 = (f32[26,16,1024]{2,1,0:T(8,128)}, f32[26,16,1024]{2,1,0:T(8,128)S(1)}, u32[]{:S(2)}, u32[]{:S(2)}) collective-permute-start(f32[26,16,1024]{2,1,0:T(8,128)} %get-tuple-element.17), channel_id=1, source_target_pairs={{4,0},{8,4},{12,8},{16,12},{20,16},{24,20},{28,24},{32,28},{36,32}... | collective-permute-start | bytes 5111816 | tf_op jit(solution)/shard_map/ppermute | solution.py:530
  7.1 26.0 %collective-permute-start.1 = (f32[26,16,1024]{2,1,0:T(8,128)}, f32[26,16,1024]{2,1,0:T(8,128)}, u32[]{:S(2)}, u32[]{:S(2)}) collective-permute-start(f32[26,16,1024]{2,1,0:T(8,128)} %get-tuple-element.13.unused_low), channel_id=1, source_target_pairs={{0,4},{4,8},{8,12},{12,16},{16,20},{20,24},{24,28},{28,32},{32,36}... | collective-permute-start | bytes 5111816 | tf_op jit(solution)/shard_map/ppermute | solution.py:529
  18.1 1.4 %collective-permute-start = (f32[8,128]{1,0:T(8,128)S(1)}, f32[8,128]{1,0:T(8,128)S(1)}, u32[]{:S(2)}, u32[]{:S(2)}) collective-permute-start(f32[8,128]{1,0:T(8,128)S(1)} %get-tuple-element.14), channel_id=1, source_target_pairs={{0,4},{4,0},{8,12},{12,8},{16,20},{20,16},{24,28},{28,24},{32,36},... | collective-permute-start | bytes 12296 | tf_op jit(solution)/shard_map/ppermute | solution.py:528
  19.6 23.6 %copy-start = (f32[160,64]{1,0:T(8,128)S(1)}, f32[160,64]{1,0:T(8,128)}, u32[]{:S(2)}) copy-start(f32[160,64]{1,0:T(8,128)} %constant.4.clone.pick) | copy-start | bytes 122884
  19.6 23.6 %copy-start.2 = (f32[2,10]{1,0:T(2,128)S(1)}, f32[2,10]{1,0:T(2,128)}, u32[]{:S(2)}) copy-start(f32[2,10]{1,0:T(2,128)} %v0.1) | copy-start | bytes 244
  20.3 22.8 %all-to-all-start = ((f32[64,8,128]{2,1,0:T(8,128)}), f32[64,8,128]{2,1,0:T(8,128)S(1)}, u32[]{:S(2)}, u32[]{:S(2)}) async-start(f32[64,8,128]{2,1,0:T(8,128)} %broadcast_in_dim.2), calls=%async_computation | async-start | bytes 524288 | tf_op jit(solution)/shard_map/all_to_all | solution.py:536
  33.0 1.2 %copy-start.3 = (f32[26,16,1024]{2,1,0:T(8,128)}, f32[26,16,1024]{2,1,0:T(8,128)S(1)}, u32[]{:S(2)}) copy-start(f32[26,16,1024]{2,1,0:T(8,128)S(1)} %collective-permute-done.2.below) | copy-start | bytes 5111812
  43.1 35.0 %copy-start.1 = (f32[128,64]{1,0:T(8,128)S(1)}, f32[128,64]{1,0:T(8,128)}, u32[]{:S(2)}) copy-start(f32[128,64]{1,0:T(8,128)} %constant.5.clone.pick) | copy-start | bytes 98308
